TPU v7x, 8 devices: a whole 2x2x1 slice. The times are simulated.
8 devices in a mesh: fsdp: 8 (over z, y, x, core).
Axes of the slice: x: 2, y: 2, z: 1, core: 2. Of those that a mesh axis runs over, the one named last changes fastest.
Arguments:
- x_layers: bfloat16 [2, 8, 2048, 768], P(None, 'fsdp')
- dy_top: bfloat16 [8, 2048, 768], P('fsdp')
- x_next: bfloat16 [8, 2048, 768], P('fsdp')
- w_up: bfloat16 [2, 768, 3072], replicated
- w_down: bfloat16 [2, 3072, 768], replicated
- acc_up: float32 [2, 768, 3072], P(None, 'fsdp')
- acc_down: float32 [2, 3072, 768], P(None, 'fsdp')
- master_up: float32 [2, 768, 3072], P(None, 'fsdp')
- master_down: float32 [2, 3072, 768], P(None, 'fsdp')
- mom_up: float32 [2, 768, 3072], P(None, 'fsdp')
- mom_down: float32 [2, 3072, 768], P(None, 'fsdp')
- var_up: float32 [2, 768, 3072], P(None, 'fsdp')
- var_down: float32 [2, 3072, 768], P(None, 'fsdp')
Outputs:
- output 1: float32 [2, 768, 3072], P(None, 'fsdp')
- output 2: float32 [2, 3072, 768], P(None, 'fsdp')
- output 3: float32 [2, 768, 3072], P(None, 'fsdp')
- output 4: float32 [2, 3072, 768], P(None, 'fsdp')
- output 5: float32 [2, 768, 3072], P(None, 'fsdp')
- output 6: float32 [2, 3072, 768], P(None, 'fsdp')
- output 7: bfloat16 [8, 2048, 768], P('fsdp')
All inputs are finite; a program needn't handle non-finite values.
Results may differ from a plain program's by a relative error of at most 0.00889.
Values are sent between devices in bfloat16 or wider.
A program may use at most 1 GiB of HBM per device.

v0:
```python
import jax
import jax.numpy as jnp
from jax import lax
from jax.sharding import PartitionSpec as P

MICRO_STEPS = 2
STEP_COUNT = 3
BETA_MOM = 0.9
BETA_VAR = 0.999
ADAM_EPS = 1e-6
WEIGHT_DECAY = 0.01
LEARN_RATE = 0.06


def lamb_update(grad_full, master, mom_prev, var_prev):
    mom_new = BETA_MOM * mom_prev + (1.0 - BETA_MOM) * grad_full
    var_new = BETA_VAR * var_prev + (1.0 - BETA_VAR) * grad_full * grad_full
    update = (mom_new / (1.0 - BETA_MOM ** STEP_COUNT)) / (jnp.sqrt(var_new / (1.0 - BETA_VAR ** STEP_COUNT)) + ADAM_EPS) + WEIGHT_DECAY * master
    return mom_new, var_new, update


def layer_backward(x_cur, d_cur, w_up_l, w_down_l, need_dx):
    pre_act = jnp.einsum('bsd,df->bsf', x_cur, w_up_l, preferred_element_type=jnp.float32)
    act_f32, gelu_vjp = jax.vjp(jax.nn.gelu, pre_act)
    act_bf = act_f32.astype(jnp.bfloat16)
    d_act = jnp.einsum('bsd,fd->bsf', d_cur, w_down_l, preferred_element_type=jnp.float32)
    d_pre = gelu_vjp(d_act)[0].astype(jnp.bfloat16)
    part_down = jnp.einsum('bsf,bsd->fd', act_bf, d_cur, preferred_element_type=jnp.float32).astype(jnp.bfloat16)
    part_up = jnp.einsum('bsd,bsf->df', x_cur, d_pre, preferred_element_type=jnp.float32).astype(jnp.bfloat16)
    d_next = None
    if need_dx:
        d_next = (d_cur.astype(jnp.float32) + jnp.einsum('bsf,df->bsd', d_pre, w_up_l, preferred_element_type=jnp.float32)).astype(jnp.bfloat16)
    return part_up, part_down, d_next


def solution(mesh):
    shard_rows = P(None, 'fsdp')
    shard_batch = P('fsdp')
    spec_whole = P()

    def local_step(x_layers, dy_top, x_next, w_up, w_down, acc_up, acc_down, master_up, master_down, mom_up, mom_down, var_up, var_down):
        layers = w_up.shape[0]
        results = [None] * layers
        new_weights = [None] * layers
        d_cur = dy_top
        for layer_id in reversed(range(layers)):
            part_up, part_down, d_cur = layer_backward(x_layers[layer_id], d_cur, w_up[layer_id], w_down[layer_id], layer_id > 0)
            sum_up = lax.psum_scatter(part_up, 'fsdp', scatter_dimension=0, tiled=True)
            sum_down = lax.psum_scatter(part_down, 'fsdp', scatter_dimension=0, tiled=True)
            grad_up = (acc_up[layer_id] + sum_up.astype(jnp.float32)) / MICRO_STEPS
            grad_down = (acc_down[layer_id] + sum_down.astype(jnp.float32)) / MICRO_STEPS
            mom_up_new, var_up_new, upd_up = lamb_update(grad_up, master_up[layer_id], mom_up[layer_id], var_up[layer_id])
            mom_down_new, var_down_new, upd_down = lamb_update(grad_down, master_down[layer_id], mom_down[layer_id], var_down[layer_id])
            sq_local = jnp.stack([jnp.sum(master_up[layer_id] * master_up[layer_id]), jnp.sum(upd_up * upd_up), jnp.sum(master_down[layer_id] * master_down[layer_id]), jnp.sum(upd_down * upd_down)])
            sq_total = lax.psum(sq_local, 'fsdp')
            up_new = master_up[layer_id] - LEARN_RATE * jnp.sqrt(sq_total[0] / sq_total[1]) * upd_up
            down_new = master_down[layer_id] - LEARN_RATE * jnp.sqrt(sq_total[2] / sq_total[3]) * upd_down
            results[layer_id] = (up_new, down_new, mom_up_new, mom_down_new, var_up_new, var_down_new)
            w_up_new = lax.all_gather(up_new.astype(jnp.bfloat16), 'fsdp', axis=0, tiled=True)
            w_down_new = lax.all_gather(down_new.astype(jnp.bfloat16), 'fsdp', axis=0, tiled=True)
            new_weights[layer_id] = (w_up_new, w_down_new)
        x_cur = x_next
        for layer_id in range(layers):
            pre_act = jnp.einsum('bsd,df->bsf', x_cur, new_weights[layer_id][0], preferred_element_type=jnp.float32)
            act_bf = jax.nn.gelu(pre_act).astype(jnp.bfloat16)
            mlp_out = jnp.einsum('bsf,fd->bsd', act_bf, new_weights[layer_id][1], preferred_element_type=jnp.float32)
            x_cur = (x_cur.astype(jnp.float32) + mlp_out).astype(jnp.bfloat16)
        stacked = tuple(jnp.stack([results[layer_id][field_id] for layer_id in range(layers)]) for field_id in range(6))
        return stacked + (x_cur,)

    return jax.shard_map(local_step, mesh=mesh, in_specs=(shard_rows, shard_batch, shard_batch, spec_whole, spec_whole) + (shard_rows,) * 8, out_specs=(shard_rows,) * 6 + (shard_batch,), check_vma=False)
```

profile of v0, /device:TPU:0, one launch (start us, length us, event | category | flops | bytes accessed | tf_op | source)
XLA Modules:
  0.0 488.6 jit_solution(2371640135302144294)
XLA Ops:
  7.2 17.5 %fusion.55 = f32[2048,3072]{1,0:T(8,128)} fusion(bf16[2,768,3072]{2,1,0:T(8,128)(2,1)} %param.16, bf16[2,1,2048,768]{3,2,1,0:T(8,128)(2,1)} %param.13), kind=kOutput, calls=%fused_computation.60 | convolution fusion | flops 9663676416 | bytes 33030144 | tf_op jit(solution)/shard_map/bsd,df->bsf/dot_general | solution.py:23
  24.8 28.8 %fusion.6 = bf16[2048,3072]{1,0:T(8,128)(2,1)} fusion(f32[2048,3072]{1,0:T(8,128)} %fusion.55, bf16[2,3072,768]{2,1,0:T(8,128)(2,1)S(1)} %copy-done.7, bf16[1,2048,768]{2,1,0:T(8,128)(2,1)S(1)} %copy-done.8), kind=kOutput, calls=%fused_computation.12 | convolution fusion | flops 9789505536 | bytes 45613056 | tf_op jit(solution)/shard_map/bsd,fd->bsf/dot_general | solution.py:26
  53.5 15.7 %fusion.70 = bf16[768,3072]{0,1:T(8,128)(2,1)} fusion(bf16[2048,3072]{1,0:T(8,128)(2,1)} %fusion.6, bf16[2,1,2048,768]{3,2,1,0:T(8,128)(2,1)} %param.13), kind=kOutput, calls=%fused_computation.68 | convolution fusion | flops 9666035712 | bytes 20447232 | tf_op jit(solution)/shard_map/bsd,bsf->df/dot_general | solution.py:29
  69.3 6.6 %copy.49 = bf16[768,3072]{1,0:T(8,128)(2,1)} copy(bf16[768,3072]{0,1:T(8,128)(2,1)} %fusion.70) | data formatting | bytes 9437184
  76.0 17.7 %fusion.49 = f32[2048,3072]{1,0:T(8,128)} fusion(bf16[2,768,3072]{2,1,0:T(8,128)(2,1)} %param.16, bf16[2,1,2048,768]{3,2,1,0:T(8,128)(2,1)} %param.13), kind=kOutput, calls=%fused_computation.55 | convolution fusion | flops 9663676416 | bytes 33030144 | tf_op jit(solution)/shard_map/bsd,df->bsf/dot_general | solution.py:23
  93.7 14.3 %fusion.43 = bf16[1,2048,768]{2,1,0:T(8,128)(2,1)S(1)} fusion(bf16[1,2048,768]{2,1,0:T(8,128)(2,1)S(1)} %copy-done.8, bf16[2048,3072]{1,0:T(8,128)(2,1)} %fusion.6, bf16[2,768,3072]{2,1,0:T(8,128)(2,1)} %param.16), kind=kOutput, calls=%fused_computation.50 | convolution fusion | flops 9668395008 | bytes 23592960 | tf_op jit(solution)/shard_map/bsf,df->bsd/dot_general | solution.py:32
  108.1 1.7 copy-done.10
  109.7 20.6 %fusion.48 = bf16[3072,768]{1,0:T(8,128)(2,1)} fusion(f32[2048,3072]{1,0:T(8,128)} %fusion.49, bf16[1,2048,768]{2,1,0:T(8,128)(2,1)S(1)} %fusion.43), kind=kOutput, calls=%fused_computation.53 | convolution fusion | flops 9722658816 | bytes 33030144 | tf_op jit(solution)/shard_map/bsf,bsd->fd/dot_general | solution.py:28
  130.4 20.1 %fusion.47 = bf16[3072,768]{1,0:T(8,128)(2,1)} fusion(f32[2048,3072]{1,0:T(8,128)} %fusion.55, bf16[1,2048,768]{2,1,0:T(8,128)(2,1)S(1)} %copy-done.8), kind=kOutput, calls=%fused_computation.52 | convolution fusion | flops 9722658816 | bytes 33030144 | tf_op jit(solution)/shard_map/bsf,bsd->fd/dot_general | solution.py:28
  150.6 1.8 copy-done.11
  152.4 39.9 %fusion.65 = bf16[768,3072]{0,1:T(8,128)(2,1)} fusion(f32[2048,3072]{1,0:T(8,128)} %fusion.49, bf16[2,3072,768]{2,1,0:T(8,128)(2,1)} %param.17, bf16[1,2048,768]{2,1,0:T(8,128)(2,1)S(1)} %copy-done.11, bf16[2,1,2048,768]{3,2,1,0:T(8,128)(2,1)} %param.13), kind=kOutput, calls=%fused_computation.67 | convolution fusion | flops 19455541248 | bytes 40894464 | tf_op jit(solution)/shard_map/bsd,bsf->df/dot_general | solution.py:29
  192.3 6.6 %copy.47 = bf16[768,3072]{1,0:T(8,128)(2,1)} copy(bf16[768,3072]{0,1:T(8,128)(2,1)} %fusion.65) | data formatting | bytes 9437184
  199.4 1.8 fusion.147
  201.2 1.6 copy.55
  202.8 1.8 fusion.146
  204.6 1.6 copy.58
  206.2 2.8 fusion.145
  209.0 2.9 copy.57
  211.9 3.3 fusion.144
  215.2 2.9 copy.56
  218.1 1.6 copy.51
  219.7 1.6 copy.54
  221.3 1.6 copy.53
  222.9 3.0 copy.52
  228.3 6.7 %multiply_reduce_fusion = (f32[]{:T(128)}, f32[96,3072]{0,1:T(8,128)}, f32[1,96,3072]{1,2,0:T(8,128)}, f32[1,96,3072]{1,2,0:T(8,128)}, f32[]{:T(128)}) fusion(f32[1,96,3072]{1,2,0:T(8,128)} %copy.55, f32[1,96,3072]{1,2,0:T(8,128)} %copy.58, bf16[96,3072]{0,1:T(8,128)(2,1)S(1)} %copy.50, f32[1,96,3072]{1,2,0:T(8,128)} %copy.57, f32[1,96,3072]{1,2,0:T(8,128)} %copy.56), kind=kLoop, calls=%fused_computation.107 | loop fusion | flops 5898238 | bytes 8847368 | tf_op jit(solution)/shard_map/reduce_sum | solution.py:54
  235.0 6.7 %multiply_reduce_fusion.3 = (f32[]{:T(128)}, f32[384,768]{1,0:T(8,128)S(1)}, f32[]{:T(128)}, f32[384,768]{1,0:T(8,128)}, f32[1,384,768]{2,1,0:T(8,128)}, /*index...) fusion(f32[2,384,768]{2,1,0:T(8,128)S(1)} %copy-done, f32[2,384,768]{2,1,0:T(8,128)} %param.25, ...), kind=kLoop, calls=%fused_computation.126 | loop fusion | flops 10616830 | bytes 17694728 | tf_op jit(solution)/shard_map/reduce_sum | solution.py:54
  241.7 2.6 pad_maximum_fusion.7
  244.3 30.7 %reduce-scatter.13.cloned.1.call-done = bf16[96,3072]{1,0:T(8,128)(2,1)} async-done(((bf16[768,3072]{1,0:T(8,128)(2,1)}), bf16[96,3072]{1,0:T(8,128)(2,1)}) %reduce-scatter.13.cloned.1.call-update) | async-done | bytes 589840
  275.0 2.2 copy.48
  277.2 7.0 %multiply_reduce_fusion.1 = (f32[]{:T(128)}, f32[96,3072]{0,1:T(8,128)}, f32[1,96,3072]{1,2,0:T(8,128)}, f32[1,96,3072]{1,2,0:T(8,128)}, f32[]{:T(128)}) fusion(f32[1,96,3072]{1,2,0:T(8,128)} %copy.51, f32[1,96,3072]{1,2,0:T(8,128)} %copy.54, bf16[96,3072]{0,1:T(8,128)(2,1)} %copy.48, f32[1,96,3072]{1,2,0:T(8,128)} %copy.53, f32[1,96,3072]{1,2,0:T(8,128)} %copy.52), kind=kLoop, calls=%fused_computation.108 | loop fusion | flops 5898238 | bytes 8847368 | tf_op jit(solution)/shard_map/reduce_sum | solution.py:54
  284.2 2.6 pad_maximum_fusion.6
  286.8 22.2 %all-reduce = (f32[4]{0:T(128)S(1)}, f32[4]{0:T(128)S(1)}) all-reduce(f32[4]{0:T(128)S(1)} %pad_maximum_fusion.7, f32[4]{0:T(128)S(1)} %pad_maximum_fusion.6), channel_id=1, replica_groups=mesh['fsdp'=8] {'fsdp'}, use_global_device_ids=true, to_apply=%region_13.0 | all-reduce | flops 8 | bytes 64 | tf_op jit(solution)/shard_map/psum | solution.py:55
  312.4 3.2 fusion.108
  317.1 3.6 fusion.102
  320.8 2.2 copy.40
  326.7 2.2 copy.42
  329.0 2.1 pad_maximum_fusion
  331.1 2.2 copy.43
  333.2 4.9 %pad_maximum_fusion.1 = (f32[2,96,3072]{1,2,0:T(8,128)}, f32[2,96,3072]{1,2,0:T(8,128)S(1)}) fusion(f32[1,96,3072]{1,2,0:T(8,128)} %get-tuple-element.42, f32[1,96,3072]{1,2,0:T(8,128)} %get-tuple-element.40, f32[1,96,3072]{1,2,0:T(8,128)} %get-tuple-element.41, f32[1,96,3072]{1,2,0:T(8,128)} %get-tuple-element.39), kind=kLoop, calls=%fused_computation.72 | loop fusion | flops 1179648 | bytes 9437184 | tf_op jit(solution)/shard_map/stack | solution.py:68
  338.1 3.4 copy.44
  341.5 2.3 copy.45
  343.9 3.3 pad_maximum_fusion.3
  347.2 2.6 pad_maximum_fusion.4
  350.5 34.6 %all-gather.5.cloned.1.call-done = bf16[768,3072]{1,0:T(8,128)(2,1)} async-done(((bf16[96,3072]{1,0:T(8,128)(2,1)}), bf16[768,3072]{1,0:T(8,128)(2,1)}) %all-gather.5.cloned.1.call-update) | async-done | bytes 4718608 | tf_op jit(solution)/shard_map/all_gather | solution.py:59
  385.1 27.8 %fusion.42 = bf16[1,2048,768]{2,1,0:T(8,128)(2,1)} fusion(bf16[1,2048,768]{2,1,0:T(8,128)(2,1)S(1)} %copy-done.9, bf16[3072,768]{1,0:T(8,128)(2,1)} %all-gather.7.cloned.1.call-done, bf16[768,3072]{1,0:T(8,128)(2,1)} %all-gather.5.cloned.1.call-done), kind=kOutput, calls=%fused_computation.48 | convolution fusion | flops 19388694528 | bytes 15728640 | tf_op jit(solution)/shard_map/bsf,fd->bsd/dot_general | solution.py:66
  412.9 7.0 %all-gather.11.cloned.1.call-done = bf16[3072,768]{1,0:T(8,128)(2,1)} async-done(((bf16[384,768]{1,0:T(8,128)(2,1)}), bf16[3072,768]{1,0:T(8,128)(2,1)}) %all-gather.11.cloned.1.call-update) | async-done | bytes 4718608 | tf_op jit(solution)/shard_map/all_gather | solution.py:60
  419.9 34.8 %all-gather.9.cloned.1.call-done = bf16[768,3072]{1,0:T(8,128)(2,1)} async-done(((bf16[96,3072]{1,0:T(8,128)(2,1)}), bf16[768,3072]{1,0:T(8,128)(2,1)}) %all-gather.9.cloned.1.call-update) | async-done | bytes 4718608 | tf_op jit(solution)/shard_map/all_gather | solution.py:59
  454.7 26.6 %fusion.41 = bf16[1,2048,768]{2,1,0:T(8,128)(2,1)} fusion(bf16[1,2048,768]{2,1,0:T(8,128)(2,1)} %fusion.42, bf16[3072,768]{1,0:T(8,128)(2,1)} %all-gather.11.cloned.1.call-done, bf16[768,3072]{1,0:T(8,128)(2,1)} %all-gather.9.cloned.1.call-done), kind=kOutput, calls=%fused_computation.46 | convolution fusion | flops 19388694528 | bytes 15728640 | tf_op jit(solution)/shard_map/bsf,fd->bsd/dot_general | solution.py:66
  (46 shorter events, 6.9 us)
Async XLA Ops:
  7.2 17.6 %copy-start.8 = (bf16[1,2048,768]{2,1,0:T(8,128)(2,1)S(1)}, bf16[1,2048,768]{2,1,0:T(8,128)(2,1)}, u32[]{:S(2)}) copy-start(bf16[1,2048,768]{2,1,0:T(8,128)(2,1)} %param.14) | copy-start | bytes 9437188
  7.2 219.7 %reduce-scatter.15.cloned.1.call-start = ((), (), s32[]{:S(2)}) async-start(), calls=%async_computation.11 | async-start | bytes 5308416
  7.2 17.6 %copy-start.7 = (bf16[2,3072,768]{2,1,0:T(8,128)(2,1)S(1)}, bf16[2,3072,768]{2,1,0:T(8,128)(2,1)}, u32[]{:S(2)}) copy-start(bf16[2,3072,768]{2,1,0:T(8,128)(2,1)} %param.17) | copy-start | bytes 28311556
  75.9 159.1 %reduce-scatter.9.cloned.1.call-start = ((), (), s32[]{:S(2)}) async-start(), calls=%async_computation.4 | async-start | bytes 5308416 | tf_op jit(solution)/shard_map/reduce_scatter | solution.py:49
  108.0 1.7 copy-start.10
  130.4 104.7 %reduce-scatter.11.cloned.1.call-start = ((), (), s32[]{:S(2)}) async-start(), calls=%async_computation.5 | async-start | bytes 5308416 | tf_op jit(solution)/shard_map/reduce_scatter | solution.py:49
  150.5 1.9 copy-start.11
  150.6 124.5 %reduce-scatter.13.cloned.1.call-start = ((), (), s32[]{:S(2)}) async-start(), calls=%async_computation.10 | async-start | bytes 5308416
  198.9 151.6 %all-gather.7.cloned.1.call-start = ((), (), s32[]{:S(2)}) async-start(), calls=%async_computation.7 | async-start | bytes 5308416 | tf_op jit(solution)/shard_map/all_gather | solution.py:60
  221.3 4.6 copy-start
  315.7 69.5 %all-gather.5.cloned.1.call-start = ((), (), s32[]{:S(2)}) async-start(), calls=%async_computation.6 | async-start | bytes 5308416 | tf_op jit(solution)/shard_map/all_gather | solution.py:59
  317.1 8.0 %copy-start.1 = (f32[1,96,3072]{1,2,0:T(8,128)S(1)}, f32[1,96,3072]{1,2,0:T(8,128)}, u32[]{:S(2)}) copy-start(f32[1,96,3072]{1,2,0:T(8,128)} %copy.55) | copy-start | bytes 3538948
  317.1 8.0 %copy-start.2 = (f32[96,3072]{0,1:T(8,128)S(1)}, f32[96,3072]{0,1:T(8,128)}, u32[]{:S(2)}) copy-start(f32[96,3072]{0,1:T(8,128)} %get-tuple-element.30) | copy-start | bytes 3538948
  323.0 96.9 %all-gather.11.cloned.1.call-start = ((), (), s32[]{:S(2)}) async-start(), calls=%async_computation.9 | async-start | bytes 5308416 | tf_op jit(solution)/shard_map/all_gather | solution.py:60
  323.8 131.0 %all-gather.9.cloned.1.call-start = ((), (), s32[]{:S(2)}) async-start(), calls=%async_computation.8 | async-start | bytes 5308416 | tf_op jit(solution)/shard_map/all_gather | solution.py:59
  343.8 3.4 copy-start.3
  343.8 3.4 copy-start.4
  343.9 3.4 copy-start.5
  343.9 3.4 copy-start.6
  347.2 37.9 %copy-start.9 = (bf16[1,2048,768]{2,1,0:T(8,128)(2,1)S(1)}, bf16[1,2048,768]{2,1,0:T(8,128)(2,1)}, u32[]{:S(2)}) copy-start(bf16[1,2048,768]{2,1,0:T(8,128)(2,1)} %param.15) | copy-start | bytes 9437188
Sparse Core Ops, SparseCore 0:
  76.1 47.8 reduce-scatter.14
  130.5 47.8 reduce-scatter.8
  181.7 44.9 reduce-scatter.10
  230.0 44.9 reduce-scatter.12
  315.8 34.6 all-gather.6
  352.2 32.9 all-gather.4
  387.0 32.9 all-gather.10
  421.7 32.9 all-gather.8
where the time goes:
time: 495 us; the launch traced here: 489 us
  matrix products  229 us (46%)
  waiting for transfers between devices  109 us (22%)
  local copies, waits for them, and re-layouts  59.9 us (12%)
  other arithmetic  48 us (10%)
  blocking collectives  22.2 us (4%)
  between operations  20.1 us (4%)
    all_gather x2, waiting for transfers between devices, local_step(): lax.all_gather(up_new.astype(jnp.bfloat16), 'fsdp', axis=0, tiled=True)  69.4 us
    dot_general x2, matrix products, layer_backward(): jnp.einsum('bsd,bsf->df', x_cur, d_pre, preferred_element_type=jnp.float32)  55.6 us
    dot_general x2, matrix products, local_step(): jnp.einsum('bsf,fd->bsd', act_bf, new_weights[layer_id][1], preferred_ele...  54.4 us
    unnamed x39, local copies, waits for them, and re-layouts  45.1 us
    dot_general x2, matrix products, layer_backward(): jnp.einsum('bsf,bsd->fd', act_bf, d_cur, preferred_element_type=jnp.float32)  40.7 us
    dot_general x2, matrix products, layer_backward(): jnp.einsum('bsd,df->bsf', x_cur, w_up_l, preferred_element_type=jnp.float32)  35.3 us
    unnamed x10, waiting for transfers between devices  31.5 us
    dot_general x1, matrix products, layer_backward(): jnp.einsum('bsd,fd->bsf', d_cur, w_down_l, preferred_element_type=jnp.flo...  28.8 us
  transfers between devices with their start and end apart: 8, of which 5 were waited for; matrix products, arithmetic and copies ran while one was open for 46% of the time, Pallas kernels for 0%

commit v1 on v0

v1 whole, which is shorter than its diff:
```python
import functools

import jax
import jax.numpy as jnp
from jax import lax
from jax.experimental import pallas as pl
from jax.experimental.pallas import tpu as pltpu
from jax.sharding import PartitionSpec as P

MICRO_STEPS = 2
STEP_COUNT = 3
BETA_MOM = 0.9
BETA_VAR = 0.999
ADAM_EPS = 1e-6
WEIGHT_DECAY = 0.01
LEARN_RATE = 0.06

C0 = 0.7978845608028654
C1 = C0 * 0.044715
MESH = pl.DeviceIdType.MESH
BF16 = jnp.bfloat16
F32 = jnp.float32
VMEM_MAX = 67043328

TOK = 2048
D = 768
FF = 3072
SUB = 128
CH = 8 * SUB
TT = 256
NT_DIMS = (((1,), (1,)), ((), ()))
NN_DIMS = (((1,), (0,)), ((), ()))


def position():
    me = lax.axis_index('fsdp')
    y, x, c = me // 4, (me // 2) % 2, me % 2
    return me, y, x, c, me + 1 - 2 * c, me + 2 - 4 * x, me + 4 - 8 * y


def entry_barrier(targets):
    barrier = pltpu.get_barrier_semaphore()
    for dev in targets:
        pl.semaphore_signal(barrier, inc=1, device_id=(dev,), device_id_type=MESH)
    pl.semaphore_wait(barrier, len(targets))


def dot(a, b, dims=NN_DIMS):
    return lax.dot_general(a, b, dims, preferred_element_type=F32)


def backward_kernel(x_hbm, dy_hbm, w1_hbm, w2_hbm, g1_ref, g2_ref,
                    xb, dyb, xt, dxacc, w1b, w2b, at, dhb, p1, p2, r01, r02, r1a1, r1b1, r1a2, r1b2, r2a1, r2b1, r2a2, r2b2,
                    ld_sem, w_sem, snd, rcv):
    me, y, x, c, partner, xn, yn = position()

    def w_copies(g, slot):
        layer = 1 - g // 3
        k = g % 3
        out = []
        for cc in range(2):
            for q in range(4):
                i = cc * 4 + q
                f0 = pl.multiple_of((2 * q + cc) * 384 + k * SUB, SUB)
                out.append(pltpu.make_async_copy(w1_hbm.at[layer, :, pl.ds(f0, SUB)], w1b.at[slot, :, pl.ds(i * SUB, SUB)], w_sem.at[slot, i]))
                out.append(pltpu.make_async_copy(w2_hbm.at[layer, pl.ds(f0, SUB), :], w2b.at[slot, pl.ds(i * SUB, SUB), :], w_sem.at[slot, 8 + i]))
        return out

    loads = [pltpu.make_async_copy(x_hbm.at[1], xb.at[1], ld_sem.at[0]),
             pltpu.make_async_copy(dy_hbm, dyb, ld_sem.at[1]),
             pltpu.make_async_copy(x_hbm.at[0], xb.at[0], ld_sem.at[2])]
    for cp in loads[:2]:
        cp.start()
    for cp in w_copies(0, 0):
        cp.start()
    loads[2].start()

    entry_barrier((partner, xn, yn))

    units = ((p1, r01, r1a1, r1b1, r2a1, r2b1, 48), (p2, r02, r1a2, r1b2, r2a2, r2b2, 64))

    def remote(src, dst, u, slot, stage, dev):
        return pltpu.make_async_remote_copy(src_ref=src, dst_ref=dst, send_sem=snd.at[u, slot, stage], recv_sem=rcv.at[u, slot, stage], device_id=(dev,), device_id_type=MESH)

    def s0(u, slot):
        p, r0, r1a, r1b, r2a, r2b, hr = units[u]
        return remote(p.at[slot, 1 - c], r0.at[slot], u, slot, 0, partner)

    def s1(u, slot):
        p, r0, r1a, r1b, r2a, r2b, hr = units[u]
        return (remote(p.at[slot, c, :, 1 - x, pl.ds(0, hr)], r1a.at[slot], u, slot, 1, xn),
                remote(p.at[slot, c, 1 - y, :, pl.ds(hr, hr)], r1b.at[slot], u, slot, 2, yn))

    def s2(u, slot):
        p, r0, r1a, r1b, r2a, r2b, hr = units[u]
        return (remote(p.at[slot, c, 1 - y, x, pl.ds(0, hr)], r2a.at[slot], u, slot, 3, yn),
                remote(p.at[slot, c, y, 1 - x, pl.ds(hr, hr)], r2b.at[slot], u, slot, 4, xn))

    def start_s0(u, slot):
        s0(u, slot).start()

    def to_s1(u, slot):
        p, r0, r1a, r1b, r2a, r2b, hr = units[u]
        s0(u, slot).wait()

        @pl.loop(0, 2)
        def _(yy):
            for xx in range(2):
                p[slot, c, yy, xx] = (p[slot, c, yy, xx].astype(F32) + r0[slot, yy, xx].astype(F32)).astype(BF16)

        for cp in s1(u, slot):
            cp.start()

    def to_s2(u, slot):
        p, r0, r1a, r1b, r2a, r2b, hr = units[u]
        ca, cb = s1(u, slot)
        ca.wait()
        for i in range(2):
            p[slot, c, i, x, 0:hr] = (p[slot, c, i, x, 0:hr].astype(F32) + r1a[slot, i].astype(F32)).astype(BF16)
        cb.wait()
        for i in range(2):
            p[slot, c, y, i, hr:2 * hr] = (p[slot, c, y, i, hr:2 * hr].astype(F32) + r1b[slot, i].astype(F32)).astype(BF16)
        for cp in s2(u, slot):
            cp.start()

    def finish(u, slot, g):
        p, r0, r1a, r1b, r2a, r2b, hr = units[u]
        layer = 1 - g // 3
        k = g % 3
        ca, cb = s2(u, slot)
        for half, (cp, r2) in enumerate(((ca, r2a), (cb, r2b))):
            cp.wait()
            rows = slice(half * hr, half * hr + hr)
            total = p[slot, c, y, x, rows].astype(F32) + r2[slot].astype(F32)
            if u == 1:
                g2_ref[layer, pl.ds(pl.multiple_of(k * SUB + half * hr, 64), hr), :] = total
            else:
                for cc in range(2):
                    for q in range(4):
                        i = cc * 4 + q
                        f0 = pl.multiple_of((2 * q + cc) * 384 + k * SUB, SUB)
                        g1_ref[layer, rows, pl.ds(f0, SUB)] = total[:, i * SUB:(i + 1) * SUB]

    loads[0].wait()
    loads[1].wait()

    @pl.loop(0, 6)
    def _(g):
        slot = g % 2
        prev = 1 - slot
        layer = 1 - g // 3
        k = g % 3
        for cp in w_copies(g, slot):
            cp.wait()

        @pl.when(g < 5)
        def _():
            for cp in w_copies(g + 1, prev):
                cp.start()

        @pl.when(g == 3)
        def _():
            loads[2].wait()

        @pl.loop(0, TOK // TT)
        def _(t):
            @pl.when((g > 0) & (t == 2))
            def _():
                to_s1(0, prev)

            @pl.when((g > 0) & (t == 5))
            def _():
                to_s2(1, prev)

            rows = pl.ds(pl.multiple_of(t * TT, TT), TT)
            xv = xb[layer, rows, :]
            dyv = dyb[rows, :]
            xt[:, rows] = xv.T
            for n in range(CH // 256):
                cs = slice(n * 256, n * 256 + 256)
                h = dot(xv, w1b[slot, :, cs])
                da = dot(dyv, w2b[slot, cs, :], NT_DIMS)
                sq = h * h
                s = 0.5 * jnp.tanh(h * (C0 + C1 * sq)) + 0.5
                a = h * s
                gp = s + a * (1.0 - s) * (2.0 * C0 + (6.0 * C1) * sq)
                at[cs, rows] = a.astype(BF16).T
                dhb[rows, cs] = (da * gp).astype(BF16)

            @pl.when(layer == 1)
            def _():
                base = jnp.where(k > 0, dxacc[rows, :], dyv.astype(F32))
                dxacc[rows, :] = base + dot(dhb[rows, :], w1b[slot], NT_DIMS)

        @pl.when(g > 0)
        def _():
            to_s2(0, prev)

        @pl.loop(0, CH // 256)
        def _(n):
            fs = pl.ds(pl.multiple_of(n * 256, 256), 256)
            res = dot(at[fs, :], dyb[...]).astype(BF16)
            p2[slot, n // 2, n % 2] = res.reshape(2, SUB, D)

        start_s0(1, slot)

        @pl.when(g > 0)
        def _():
            finish(1, prev, g - 1)

        @pl.loop(0, CH // 256)
        def _(n):
            fs = pl.ds(pl.multiple_of(n * 256, 256), 256)
            res = dot(xt[...], dhb[:, fs]).astype(BF16)
            for b in range(8):
                p1[slot, b % 2, b // 4, (b // 2) % 2, :, fs] = res[b * 96:(b + 1) * 96]

        to_s1(1, slot)
        start_s0(0, slot)

        @pl.when(g > 0)
        def _():
            finish(0, prev, g - 1)

        @pl.when(g == 2)
        def _():
            @pl.loop(0, TOK // TT)
            def _(t):
                rows = pl.ds(pl.multiple_of(t * TT, TT), TT)
                dyb[rows, :] = dxacc[rows, :].astype(BF16)

    to_s1(0, 1)
    to_s2(1, 1)
    to_s2(0, 1)
    finish(1, 1, 5)
    finish(0, 1, 5)


def run_backward(x, dy, w1, w2):
    any_spec = pl.BlockSpec(memory_space=pl.ANY)
    vm = pltpu.VMEM
    return pl.pallas_call(
        backward_kernel,
        out_shape=(jax.ShapeDtypeStruct((2, 96, FF), F32), jax.ShapeDtypeStruct((2, 384, D), F32)),
        in_specs=[any_spec] * 4,
        out_specs=(pl.BlockSpec(memory_space=vm),) * 2,
        scratch_shapes=[
            vm((2, TOK, D), BF16), vm((TOK, D), BF16), vm((D, TOK), BF16), vm((TOK, D), F32),
            vm((2, D, CH), BF16), vm((2, CH, D), BF16), vm((CH, TOK), BF16), vm((TOK, CH), BF16),
            vm((2, 2, 2, 2, 96, CH), BF16), vm((2, 2, 2, 2, SUB, D), BF16),
            vm((2, 2, 2, 96, CH), BF16), vm((2, 2, 2, SUB, D), BF16),
            vm((2, 2, 48, CH), BF16), vm((2, 2, 48, CH), BF16), vm((2, 2, 64, D), BF16), vm((2, 2, 64, D), BF16),
            vm((2, 48, CH), BF16), vm((2, 48, CH), BF16), vm((2, 64, D), BF16), vm((2, 64, D), BF16),
            pltpu.SemaphoreType.DMA((3,)), pltpu.SemaphoreType.DMA((2, 16)),
            pltpu.SemaphoreType.DMA((2, 2, 5)), pltpu.SemaphoreType.DMA((2, 2, 5)),
        ],
        compiler_params=pltpu.CompilerParams(collective_id=0, has_side_effects=True, vmem_limit_bytes=VMEM_MAX),
        name='backward',
    )(x, dy, w1, w2)


def moments_kernel(g1, a1, w1, m1, v1, g2, a2, w2, m2, v2, m1o, v1o, u1o, m2o, v2o, u2o, sq):
    first = pl.program_id(1) == 0

    @pl.when(first)
    def _():
        sq[...] = jnp.zeros_like(sq)

    def part(kind, g, acc, w, m, v, mo, vo, uo):
        grad = (acc[0] + g[0]) / MICRO_STEPS
        master = w[0]
        mom = BETA_MOM * m[0] + (1.0 - BETA_MOM) * grad
        var = BETA_VAR * v[0] + (1.0 - BETA_VAR) * grad * grad
        upd = (mom / (1.0 - BETA_MOM ** STEP_COUNT)) / (jnp.sqrt(var / (1.0 - BETA_VAR ** STEP_COUNT)) + ADAM_EPS) + WEIGHT_DECAY * master
        mo[0] = mom
        vo[0] = var
        uo[0] = upd
        for i, val in enumerate((master, upd)):
            folded = jnp.sum((val * val).reshape(-1, 8, val.shape[-1]), axis=0)
            lanes = folded[:, 0:128]
            for j in range(1, val.shape[-1] // 128):
                lanes = lanes + folded[:, j * 128:(j + 1) * 128]
            sq[0, kind * 2 + i] += lanes

    part(0, g1, a1, w1, m1, v1, m1o, v1o, u1o)
    part(1, g2, a2, w2, m2, v2, m2o, v2o, u2o)


def run_moments(g1, a1, w1, m1, v1, g2, a2, w2, m2, v2):
    up = pl.BlockSpec((1, 96, 768), lambda l, j: (l, 0, j))
    down = pl.BlockSpec((1, 96, 768), lambda l, j: (l, j, 0))
    s1 = jax.ShapeDtypeStruct((2, 96, FF), F32)
    s2 = jax.ShapeDtypeStruct((2, 384, D), F32)
    return pl.pallas_call(
        moments_kernel,
        grid=(2, 4),
        out_shape=(s1, s1, s1, s2, s2, s2, jax.ShapeDtypeStruct((2, 4, 8, 128), F32)),
        in_specs=[up] * 5 + [down] * 5,
        out_specs=(up, up, up, down, down, down, pl.BlockSpec((1, 4, 8, 128), lambda l, j: (l, 0, 0, 0))),
        name='moments',
    )(g1, a1, w1, m1, v1, g2, a2, w2, m2, v2)


def sums_kernel(sq_ref, out_ref, mine, got, snd, rcv):
    me = position()[0]
    mine[...] = jnp.sum(sq_ref[...], axis=1)
    others = [lax.rem(me + i, 8) for i in range(1, 8)]
    entry_barrier(others)
    copies = []
    for i, dev in enumerate(others):
        copies.append(pltpu.make_async_remote_copy(src_ref=mine, dst_ref=got.at[i], send_sem=snd.at[i], recv_sem=rcv.at[i], device_id=(dev,), device_id_type=MESH))
        copies[-1].start()
    got[7] = mine[...]
    for cp in copies:
        cp.wait()
    total = got[lax.rem(me + 7, 8)]
    for dev in range(1, 8):
        total = total + got[lax.rem(me + 7 - dev + 8, 8)]
    out_ref[...] = jnp.broadcast_to(jnp.sum(total, axis=1, keepdims=True), (8, 128))


def run_sums(sq):
    vmem = pl.BlockSpec(memory_space=pltpu.VMEM)
    return pl.pallas_call(
        sums_kernel,
        out_shape=jax.ShapeDtypeStruct((8, 128), F32),
        in_specs=[vmem],
        out_specs=vmem,
        scratch_shapes=[pltpu.VMEM((8, 128), F32), pltpu.VMEM((8, 8, 128), F32), pltpu.SemaphoreType.DMA((7,)), pltpu.SemaphoreType.DMA((7,))],
        compiler_params=pltpu.CompilerParams(collective_id=1, has_side_effects=True),
        name='sums',
    )(sq.reshape(8, 8, 128))


def forward_kernel(w1_hbm, w2_hbm, x_hbm, o_ref, wf1, wf2, ab, xb, ld_sem, snd, rcv):
    me, y, x, c, partner, xn, yn = position()
    fulls = (wf1.at[0], wf2.at[0], wf1.at[1], wf2.at[1])
    halves = (48, 192, 48, 192)
    srcs = (w1_hbm.at[0], w2_hbm.at[0], w1_hbm.at[1], w2_hbm.at[1])
    loads = [pltpu.make_async_copy(srcs[m], fulls[m].at[y, x, c], ld_sem.at[m]) for m in range(4)]
    loads.append(pltpu.make_async_copy(x_hbm, xb, ld_sem.at[4]))
    for cp in loads:
        cp.start()
    entry_barrier((partner, xn, yn))

    def same(ref, m, i, dev):
        return pltpu.make_async_remote_copy(src_ref=ref, dst_ref=ref, send_sem=snd.at[m, i], recv_sem=rcv.at[m, i], device_id=(dev,), device_id_type=MESH)

    def parts(m, name):
        f, h = fulls[m], halves[m]
        lo, hi = pl.ds(0, h), pl.ds(h, h)
        if name == 's1':
            return same(f.at[y, x, c, lo], m, 0, xn), same(f.at[y, x, c, hi], m, 1, yn)
        if name == 's2':
            return same(f.at[y, :, c, lo], m, 2, yn), same(f.at[:, x, c, hi], m, 3, xn)
        if name == 'd1':
            return (same(f.at[y, x, c], m, 4, partner),)
        if name == 'd2':
            return same(f.at[y, 1 - x, c, lo], m, 5, partner), same(f.at[1 - y, x, c, hi], m, 6, partner)
        return same(f.at[1 - y, :, c, lo], m, 7, partner), same(f.at[:, 1 - x, c, hi], m, 8, partner)

    def start(m, *names):
        for name in names:
            for cp in parts(m, name):
                cp.start()

    def wait(m, *names):
        for name in names:
            for cp in parts(m, name):
                cp.wait()

    def first(m):
        start(m, 's1', 'd1')

    def second(m):
        wait(m, 's1')
        start(m, 's2', 'd2')

    def third(m):
        wait(m, 's2')
        start(m, 'd3')

    def done(m):
        wait(m, 'd1', 'd2', 'd3')

    def up(layer, hook):
        @pl.loop(0, TOK // TT)
        def _(t):
            hook(t)
            rows = pl.ds(pl.multiple_of(t * TT, TT), TT)
            xv = xb[rows, :]
            for n in range(4):
                cs = slice(n * 768, n * 768 + 768)
                h = dot(xv, wf1[layer, :, :, :, :, cs].reshape(D, 768))
                s = 0.5 * jnp.tanh(h * (C0 + C1 * (h * h))) + 0.5
                ab[rows, cs] = (h * s).astype(BF16)

    def down(layer, hook):
        @pl.loop(0, TOK // TT)
        def _(t):
            hook(t)
            rows = pl.ds(pl.multiple_of(t * TT, TT), TT)
            res = xb[rows, :].astype(F32) + dot(ab[rows, :], wf2[layer].reshape(FF, D))
            if layer == 0:
                xb[rows, :] = res.astype(BF16)
            else:
                o_ref[rows, :] = res.astype(BF16)

    def no_hook(t):
        pass

    def at_step(step, fn):
        def hook(t):
            @pl.when(t == step)
            def _():
                fn()
        return hook

    def second_and_next(m):
        def fn():
            second(m)
            if m < 3:
                first(m + 1)
        return fn

    loads[0].wait()
    first(0)
    for cp in loads[1:]:
        cp.wait()
    second_and_next(0)()
    third(0)
    second_and_next(1)()
    done(0)
    up(0, no_hook)
    third(1)
    done(1)
    down(0, at_step(3, second_and_next(2)))
    third(2)
    second_and_next(3)()
    done(2)
    up(1, no_hook)
    third(3)
    done(3)
    down(1, no_hook)


def run_forward(w1, w2, x):
    any_spec = pl.BlockSpec(memory_space=pl.ANY)
    vm = pltpu.VMEM
    return pl.pallas_call(
        forward_kernel,
        out_shape=jax.ShapeDtypeStruct((TOK, D), BF16),
        in_specs=[any_spec] * 3,
        out_specs=pl.BlockSpec(memory_space=vm),
        scratch_shapes=[
            vm((2, 2, 2, 2, 96, FF), BF16), vm((2, 2, 2, 2, 384, D), BF16), vm((TOK, FF), BF16), vm((TOK, D), BF16),
            pltpu.SemaphoreType.DMA((5,)), pltpu.SemaphoreType.DMA((4, 9)), pltpu.SemaphoreType.DMA((4, 9)),
        ],
        compiler_params=pltpu.CompilerParams(collective_id=2, has_side_effects=True, vmem_limit_bytes=VMEM_MAX),
        name='forward',
    )(w1, w2, x)


def solution(mesh):
    shard_rows = P(None, 'fsdp')
    shard_batch = P('fsdp')
    spec_whole = P()

    def local_step(x_layers, dy_top, x_next, w_up, w_down, acc_up, acc_down, master_up, master_down, mom_up, mom_down, var_up, var_down):
        g1, g2 = run_backward(x_layers.reshape(2, TOK, D), dy_top.reshape(TOK, D), w_up, w_down)
        m1, v1, u1, m2, v2, u2, sq = run_moments(g1, acc_up, master_up, mom_up, var_up, g2, acc_down, master_down, mom_down, var_down)
        tot = run_sums(sq)[:, 0].reshape(2, 4)
        ratio = LEARN_RATE * jnp.sqrt(tot[:, 0::2] / tot[:, 1::2])
        up_new = master_up - ratio[:, 0][:, None, None] * u1
        down_new = master_down - ratio[:, 1][:, None, None] * u2
        out = run_forward(up_new.astype(BF16), down_new.astype(BF16), x_next.reshape(TOK, D))
        return up_new, down_new, m1, m2, v1, v2, out.reshape(1, TOK, D)

    return jax.shard_map(local_step, mesh=mesh, in_specs=(shard_rows, shard_batch, shard_batch, spec_whole, spec_whole) + (shard_rows,) * 8, out_specs=(shard_rows,) * 6 + (shard_batch,), check_vma=False)
```

time: 495 us -> 292 us (0.59); the launches traced: 489 us -> 292 us
  Pallas kernels: 0 us -> 280 us
  matrix products: 229 us -> 0 us
  waiting for transfers between devices: 109 us -> 0 us
  local copies, waits for them, and re-layouts: 59.9 us -> 5.03 us
  other arithmetic: 48 us -> 6.3 us
  blocking collectives: 22.2 us -> 0 us
  between operations: 20.1 us -> 0.7 us
    pallas_call x0 -> x4, Pallas kernels: none -> 280 us  [the longest x1 155 us: run_backward(): pl.pallas_call(backward_kernel, out_shape=(jax.ShapeDtypeStruct((2, 96, F...]
    dot_general x10 -> x0, matrix products: 229 us -> none  [the longest x2 55.6 us: layer_backward(): jnp.einsum('bsd,bsf->df', x_cur, d_pre, preferred_element_type=jnp.float32)]
    all_gather x4 -> x0, waiting for transfers between devices: 77 us -> none  [the longest x2 69.4 us: local_step(): lax.all_gather(up_new.astype(jnp.bfloat16), 'fsdp', axis=0, tiled=True)]
    unnamed x39 -> x7, local copies, waits for them, and re-layouts: 45.1 us -> 3.78 us
    unnamed x10 -> x0, waiting for transfers between devices: 31.5 us -> none
    psum x1 -> x0, blocking collectives: 22.2 us -> none  [local_step(): sq_total = lax.psum(sq_local, 'fsdp')]
    reduce_sum x4 -> x0, other arithmetic: 21.3 us -> none  [the longest x2 13.7 us: local_step(): jnp.sum(upd_up * upd_up)]
    another operation x6 -> x0, other arithmetic: 18.2 us -> none  [the longest x4 13 us: local_step(): jnp.stack([results[layer_id][field_id] for layer_id in range(layers)])]
  transfers between devices with their start and end apart: 8 -> 0, of which waited for: 5 -> 0; matrix products, arithmetic and copies ran while one was open for 46% -> 0% of each run, Pallas kernels for 0% -> 0%
where the time goes in v1:
time: 292 us
  Pallas kernels  280 us (96%)
  other arithmetic  6.3 us (2%)
  local copies, waits for them, and re-layouts  5.03 us (2%)
    pallas_call x1, Pallas kernels, run_backward(): pl.pallas_call(backward_kernel, out_shape=(jax.ShapeDtypeStruct((2, 96, F...  155 us
    pallas_call x1, Pallas kernels, run_forward(): pl.pallas_call(forward_kernel, out_shape=jax.ShapeDtypeStruct((TOK, D), B...  104 us
    pallas_call x1, Pallas kernels, run_moments(): pl.pallas_call(moments_kernel, grid=(2, 4), out_shape=(s1, s1, s1, s2, s2...  15 us
    pallas_call x1, Pallas kernels, run_sums(): pl.pallas_call(sums_kernel, out_shape=jax.ShapeDtypeStruct((8, 128), F32)...  6.11 us

profile of v1, /device:TPU:0, one launch (start us, length us, event | category | flops | bytes accessed | tf_op | source)
XLA Modules:
  0.0 292.1 jit_solution(14611865457055225358)
XLA Ops:
  0.6 154.7 %backward.1 = (f32[2,96,3072]{2,1,0:T(8,128)}, f32[2,384,768]{2,1,0:T(8,128)}) custom-call(bf16[2,2048,768]{2,1,0:T(8,128)(2,1)} %bitcast.6, bf16[2048,768]{1,0:T(8,128)(2,1)} %bitcast.7, bf16[2,768,3072]{2,1,0:T(8,128)(2,1)} %w1_hbm.1, bf16[2,3072,768]{2,1,0:T(8,128)(2,1)} %w2_hbm.1), custom_call_target="tpu_custom_call" | custom-call | tf_op jit(solution)/shard_map/backward/pallas_call | solution.py:242
  155.3 0.0 copy-start
  155.3 15.0 %moments.1 = (f32[2,96,3072]{2,1,0:T(8,128)}, f32[2,96,3072]{2,1,0:T(8,128)}, f32[2,96,3072]{2,1,0:T(8,128)}, f32[2,384,768]{2,1,0:T(8,128)}, f32[2,384,768]{2,1...) custom-call(f32[2,96,3072]{2,1,0:T(8,128)} %get-tuple-element.16.g1, f32[2,96,3072]{2,1,0:T(8,128)} %a1.1, ...), custom_call_target="tpu_custom_call" | custom-call | tf_op jit(solution)/shard_map/moments/pallas_call | solution.py:294
  170.3 6.1 %sums.1 = f32[8,128]{1,0:T(8,128)} custom-call(f32[8,8,128]{2,1,0:T(8,128)} %bitcast.9), custom_call_target="tpu_custom_call" | custom-call | tf_op jit(solution)/shard_map/sums/pallas_call | solution.py:324
  176.5 0.8 slice_reduce_fusion
  177.3 0.1 reshape_squeeze.3
  177.3 0.1 slice.17
  177.4 0.1 slice.16
  177.5 0.2 slice_reduce_fusion.1
  177.7 0.0 copy-done
  177.7 0.0 copy-start.1
  177.8 0.0 copy-start.2
  177.8 4.0 %fusion = (bf16[2,384,768]{2,1,0:T(8,128)(2,1)}, f32[2,384,768]{2,1,0:T(8,128)}) fusion(f32[2,384,768]{2,1,0:T(8,128)S(1)} %copy-done, f32[2,384,768]{2,1,0:T(8,128)} %get-tuple-element.20, f32[2]{0:T(128)S(1)} %get-tuple-element.25), kind=kLoop, calls=%fused_computation.6 | loop fusion | flops 1769472 | bytes 8257544 | tf_op jit(solution)/shard_map/convert_element_type | solution.py:476
  181.8 0.0 copy-done.1
  181.8 0.0 copy-done.2
  181.8 2.3 fusion.1
  184.1 104.2 %forward.1 = bf16[2048,768]{1,0:T(8,128)(2,1)} custom-call(bf16[2,96,3072]{2,1,0:T(8,128)(2,1)} %get-tuple-element.29.w1_hbm, bf16[2,384,768]{2,1,0:T(8,128)(2,1)} %get-tuple-element.27.w2_hbm, bf16[2048,768]{1,0:T(8,128)(2,1)} %bitcast.8), custom_call_target="tpu_custom_call" | custom-call | tf_op jit(solution)/shard_map/forward/pallas_call | solution.py:450
  288.3 3.8 %copy.21 = bf16[1,2048,768]{2,1,0:T(8,128)(2,1)} copy(bf16[1,2048,768]{2,1,0:T(8,128)(2,1)} %bitcast.5) | data formatting | bytes 6291456
  (1 shorter events, 0.0 us)
Async XLA Ops:
  155.3 22.4 %copy-start = (f32[2,384,768]{2,1,0:T(8,128)S(1)}, f32[2,384,768]{2,1,0:T(8,128)}, u32[]{:S(2)}) copy-start(f32[2,384,768]{2,1,0:T(8,128)} %w2.1) | copy-start | bytes 7077892
  177.7 4.0 %copy-start.1 = (f32[2,96,3072]{2,1,0:T(8,128)S(1)}, f32[2,96,3072]{2,1,0:T(8,128)}, u32[]{:S(2)}) copy-start(f32[2,96,3072]{2,1,0:T(8,128)} %w1.1) | copy-start | bytes 7077892
  177.8 4.0 %copy-start.2 = (f32[2,96,3072]{2,1,0:T(8,128)S(1)}, f32[2,96,3072]{2,1,0:T(8,128)}, u32[]{:S(2)}) copy-start(f32[2,96,3072]{2,1,0:T(8,128)} %get-tuple-element.19) | copy-start | bytes 7077892

commit v2 on v1

--- a/solution.py
+++ b/solution.py
@@ -49,10 +49,21 @@
     return lax.dot_general(a, b, dims, preferred_element_type=F32)
 
 
-def backward_kernel(x_hbm, dy_hbm, w1_hbm, w2_hbm, g1_ref, g2_ref,
+def moments(grad_sum, acc, master, mom_prev, var_prev):
+    grad = (acc + grad_sum) / MICRO_STEPS
+    mom = BETA_MOM * mom_prev + (1.0 - BETA_MOM) * grad
+    var = BETA_VAR * var_prev + (1.0 - BETA_VAR) * grad * grad
+    upd = (mom / (1.0 - BETA_MOM ** STEP_COUNT)) / (jnp.sqrt(var / (1.0 - BETA_VAR ** STEP_COUNT)) + ADAM_EPS) + WEIGHT_DECAY * master
+    return mom, var, upd
+
+
+def backward_kernel(x_hbm, dy_hbm, w1_hbm, w2_hbm, acc1, acc2, mas1, mas2, mom1, mom2, var1, var2,
+                    g1_ref, g2_ref, tot_ref, ws1, ws2, wg1,
                     xb, dyb, xt, dxacc, w1b, w2b, at, dhb, p1, p2, r01, r02, r1a1, r1b1, r1a2, r1b2, r2a1, r2b1, r2a2, r2b2,
-                    ld_sem, w_sem, snd, rcv):
+                    mb, sqb, smine, sgot,
+                    ld_sem, w_sem, snd, rcv, l_sem, x_snd, x_rcv, a_snd, a_rcv):
     me, y, x, c, partner, xn, yn = position()
+    others = [lax.rem(me + i, 8) for i in range(1, 8)]
 
     def w_copies(g, slot):
         layer = 1 - g // 3
@@ -75,7 +86,96 @@
         cp.start()
     loads[2].start()
 
-    entry_barrier((partner, xn, yn))
+    sqb[...] = jnp.zeros_like(sqb)
+    smine[...] = jnp.zeros_like(smine)
+    entry_barrier(others)
+
+    def lamb_loads(layer):
+        out = []
+        for a, (up, down) in enumerate(((acc1, acc2), (mom1, mom2), (var1, var2), (mas1, mas2))):
+            for j in range(8):
+                src = up.at[layer, :, pl.ds(j * 768, 768)] if j < 4 else down.at[layer, pl.ds((j - 4) * 96, 96), :]
+                dst = dxacc.at[pl.ds((a * 8 + j) * 96, 96), :] if a < 3 else mb.at[pl.ds(j * 96, 96), :]
+                out.append(pltpu.make_async_copy(src, dst, l_sem.at[a * 8 + j]))
+        return out
+
+    def lamb_moments(layer):
+        for cp in lamb_loads(layer):
+            cp.wait()
+        for kind in range(2):
+            @pl.loop(0, 4)
+            def _(j):
+                spans = [pl.ds(pl.multiple_of((a * 8 + kind * 4 + j) * 96, 96), 96) for a in range(3)]
+                grad_sum = g1_ref[layer, :, pl.ds(pl.multiple_of(j * 768, 768), 768)] if kind == 0 else g2_ref[layer, pl.ds(pl.multiple_of(j * 96, 96), 96), :]
+                master = mb[spans[0], :] if kind == 0 else mb[pl.ds(pl.multiple_of((4 + j) * 96, 96), 96), :]
+                upd = moments(grad_sum, dxacc[spans[0], :], master, dxacc[spans[1], :], dxacc[spans[2], :])[2]
+                dxacc[spans[0], :] = upd
+                for i, val in enumerate((master, upd)):
+                    folded = jnp.sum((val * val).reshape(12, 8, 768), axis=0)
+                    lanes = folded[:, 0:128]
+                    for b in range(1, 6):
+                        lanes = lanes + folded[:, b * 128:(b + 1) * 128]
+                    sqb[layer, kind * 2 + i] += lanes
+
+    def lamb_copies(layer):
+        return [pltpu.make_async_remote_copy(src_ref=smine.at[layer], dst_ref=sgot.at[layer, i], send_sem=x_snd.at[layer, i], recv_sem=x_rcv.at[layer, i], device_id=(dev,), device_id_type=MESH) for i, dev in enumerate(others)]
+
+    def lamb_send(layer):
+        for i in range(4):
+            smine[layer, i:i + 1, :] = jnp.sum(sqb[layer, i], axis=0, keepdims=True)
+        for cp in lamb_copies(layer):
+            cp.start()
+
+    def lamb_apply(layer):
+        sgot[layer, 7] = smine[layer]
+        for cp in lamb_copies(layer):
+            cp.wait()
+        total = sgot[layer, lax.rem(me + 7, 8)]
+        for dev in range(1, 8):
+            total = total + sgot[layer, lax.rem(me + 7 - dev + 8, 8)]
+        tot_ref[layer] = jnp.broadcast_to(jnp.sum(total, axis=1, keepdims=True), (8, 128))
+        for kind in range(2):
+            scale = LEARN_RATE * jnp.sqrt(tot_ref[layer, 2 * kind:2 * kind + 1, 0:1] / tot_ref[layer, 2 * kind + 1:2 * kind + 2, 0:1])
+
+            @pl.loop(0, 4)
+            def _(j):
+                span = pl.ds(pl.multiple_of((kind * 4 + j) * 96, 96), 96)
+                new = (mb[span, :] - scale * dxacc[span, :]).astype(BF16)
+                if kind == 0:
+                    ws1[layer, :, pl.ds(pl.multiple_of(j * 768, 768), 768)] = new
+                else:
+                    ws2[layer, pl.ds(pl.multiple_of(j * 96, 96), 96), :] = new
+
+    lo, hi = pl.ds(0, 48), pl.ds(48, 48)
+
+    def gather_copy(src, dst, i, dev):
+        return pltpu.make_async_remote_copy(src_ref=src, dst_ref=dst, send_sem=a_snd.at[i], recv_sem=a_rcv.at[i], device_id=(dev,), device_id_type=MESH)
+
+    def gather_local():
+        return pltpu.make_async_copy(ws1.at[1], wg1.at[y, x, c], ld_sem.at[3])
+
+    def gather_parts(name):
+        def same(ref, i, dev):
+            return gather_copy(ref, ref, i, dev)
+        if name == 's1':
+            return (gather_copy(ws1.at[1, lo], wg1.at[y, x, c, lo], 0, xn), gather_copy(ws1.at[1, hi], wg1.at[y, x, c, hi], 1, yn))
+        if name == 's2':
+            return same(wg1.at[y, :, c, lo], 2, yn), same(wg1.at[:, x, c, hi], 3, xn)
+        if name == 'd1':
+            return (gather_copy(ws1.at[1], wg1.at[y, x, c], 4, partner),)
+        if name == 'd2':
+            return same(wg1.at[y, 1 - x, c, lo], 5, partner), same(wg1.at[1 - y, x, c, hi], 6, partner)
+        return same(wg1.at[1 - y, :, c, lo], 7, partner), same(wg1.at[:, 1 - x, c, hi], 8, partner)
+
+    def gather_start(*names):
+        for name in names:
+            for cp in gather_parts(name):
+                cp.start()
+
+    def gather_wait(*names):
+        for name in names:
+            for cp in gather_parts(name):
+                cp.wait()
 
     units = ((p1, r01, r1a1, r1b1, r2a1, r2b1, 48), (p2, r02, r1a2, r1b2, r2a2, r2b2, 64))
 
@@ -161,18 +261,15 @@
         @pl.when(g == 3)
         def _():
             loads[2].wait()
-
-        @pl.loop(0, TOK // TT)
-        def _(t):
-            @pl.when((g > 0) & (t == 2))
-            def _():
-                to_s1(0, prev)
-
-            @pl.when((g > 0) & (t == 5))
-            def _():
-                to_s2(1, prev)
-
-            rows = pl.ds(pl.multiple_of(t * TT, TT), TT)
+            for cp in lamb_loads(1):
+                cp.start()
+
+        @pl.when(g == 5)
+        def _():
+            for cp in lamb_loads(0):
+                cp.start()
+
+        def tile(rows):
             xv = xb[layer, rows, :]
             dyv = dyb[rows, :]
             xt[:, rows] = xv.T
@@ -187,10 +284,46 @@
                 at[cs, rows] = a.astype(BF16).T
                 dhb[rows, cs] = (da * gp).astype(BF16)
 
-            @pl.when(layer == 1)
+        def token_loop(with_dx):
+            @pl.loop(0, TOK // (2 * TT))
+            def _(t):
+                @pl.when((g > 0) & (t == 1))
+                def _():
+                    to_s1(0, prev)
+
+                if not with_dx:
+                    @pl.when((g == 4) & (t == 2))
+                    def _():
+                        lamb_apply(1)
+                        gather_start('s1', 'd1')
+                        gather_local().start()
+
+                @pl.when((g > 0) & (t == 3))
+                def _():
+                    to_s2(1, prev)
+
+                base = pl.multiple_of(t * (2 * TT), 2 * TT)
+                spans = [pl.ds(base + i * TT, TT) for i in range(2)]
+                for rows in spans:
+                    tile(rows)
+                if with_dx:
+                    for rows in spans:
+                        dxacc[rows, :] += dot(dhb[rows, :], w1b[slot], NT_DIMS)
+
+        @pl.when(layer == 1)
+        def _():
+            @pl.when(k == 0)
             def _():
-                base = jnp.where(k > 0, dxacc[rows, :], dyv.astype(F32))
-                dxacc[rows, :] = base + dot(dhb[rows, :], w1b[slot], NT_DIMS)
+                @pl.loop(0, TOK // 128)
+                def _(t):
+                    rows = pl.ds(pl.multiple_of(t * 128, 128), 128)
+                    dxacc[rows, :] = dyb[rows, :].astype(F32)
+
+            token_loop(True)
+
+        @pl.when(layer == 0)
+        def _():
+            token_loop(False)
 
         @pl.when(g > 0)
         def _():
@@ -229,116 +362,90 @@
                 rows = pl.ds(pl.multiple_of(t * TT, TT), TT)
                 dyb[rows, :] = dxacc[rows, :].astype(BF16)
 
+        @pl.when(g == 3)
+        def _():
+            lamb_moments(1)
+            lamb_send(1)
+
+        @pl.when(g == 4)
+        def _():
+            gather_local().wait()
+            gather_wait('s1')
+            gather_start('s2', 'd2')
+
     to_s1(0, 1)
     to_s2(1, 1)
     to_s2(0, 1)
+    gather_wait('s2')
+    gather_start('d3')
     finish(1, 1, 5)
     finish(0, 1, 5)
-
-
-def run_backward(x, dy, w1, w2):
+    lamb_moments(0)
+    lamb_send(0)
+    lamb_apply(0)
+    gather_wait('d1', 'd2', 'd3')
+
+
+def run_backward(*args):
     any_spec = pl.BlockSpec(memory_space=pl.ANY)
     vm = pltpu.VMEM
     return pl.pallas_call(
         backward_kernel,
-        out_shape=(jax.ShapeDtypeStruct((2, 96, FF), F32), jax.ShapeDtypeStruct((2, 384, D), F32)),
-        in_specs=[any_spec] * 4,
-        out_specs=(pl.BlockSpec(memory_space=vm),) * 2,
+        out_shape=(jax.ShapeDtypeStruct((2, 96, FF), F32), jax.ShapeDtypeStruct((2, 384, D), F32), jax.ShapeDtypeStruct((2, 8, 128), F32),
+                   jax.ShapeDtypeStruct((2, 96, FF), BF16), jax.ShapeDtypeStruct((2, 384, D), BF16), jax.ShapeDtypeStruct((2, 2, 2, 96, FF), BF16)),
+        in_specs=[any_spec] * 12,
+        out_specs=(pl.BlockSpec(memory_space=vm),) * 5 + (any_spec,),
         scratch_shapes=[
-            vm((2, TOK, D), BF16), vm((TOK, D), BF16), vm((D, TOK), BF16), vm((TOK, D), F32),
+            vm((2, TOK, D), BF16), vm((TOK, D), BF16), vm((D, TOK), BF16), vm((24 * 96, D), F32),
             vm((2, D, CH), BF16), vm((2, CH, D), BF16), vm((CH, TOK), BF16), vm((TOK, CH), BF16),
             vm((2, 2, 2, 2, 96, CH), BF16), vm((2, 2, 2, 2, SUB, D), BF16),
             vm((2, 2, 2, 96, CH), BF16), vm((2, 2, 2, SUB, D), BF16),
             vm((2, 2, 48, CH), BF16), vm((2, 2, 48, CH), BF16), vm((2, 2, 64, D), BF16), vm((2, 2, 64, D), BF16),
             vm((2, 48, CH), BF16), vm((2, 48, CH), BF16), vm((2, 64, D), BF16), vm((2, 64, D), BF16),
-            pltpu.SemaphoreType.DMA((3,)), pltpu.SemaphoreType.DMA((2, 16)),
+            vm((768, 768), F32), vm((2, 4, 8, 128), F32), vm((2, 8, 128), F32), vm((2, 8, 8, 128), F32),
+            pltpu.SemaphoreType.DMA((4,)), pltpu.SemaphoreType.DMA((2, 16)),
             pltpu.SemaphoreType.DMA((2, 2, 5)), pltpu.SemaphoreType.DMA((2, 2, 5)),
+            pltpu.SemaphoreType.DMA((32,)), pltpu.SemaphoreType.DMA((2, 7)), pltpu.SemaphoreType.DMA((2, 7)),
+            pltpu.SemaphoreType.DMA((9,)), pltpu.SemaphoreType.DMA((9,)),
         ],
         compiler_params=pltpu.CompilerParams(collective_id=0, has_side_effects=True, vmem_limit_bytes=VMEM_MAX),
         name='backward',
-    )(x, dy, w1, w2)
-
-
-def moments_kernel(g1, a1, w1, m1, v1, g2, a2, w2, m2, v2, m1o, v1o, u1o, m2o, v2o, u2o, sq):
-    first = pl.program_id(1) == 0
-
-    @pl.when(first)
-    def _():
-        sq[...] = jnp.zeros_like(sq)
-
-    def part(kind, g, acc, w, m, v, mo, vo, uo):
-        grad = (acc[0] + g[0]) / MICRO_STEPS
-        master = w[0]
-        mom = BETA_MOM * m[0] + (1.0 - BETA_MOM) * grad
-        var = BETA_VAR * v[0] + (1.0 - BETA_VAR) * grad * grad
-        upd = (mom / (1.0 - BETA_MOM ** STEP_COUNT)) / (jnp.sqrt(var / (1.0 - BETA_VAR ** STEP_COUNT)) + ADAM_EPS) + WEIGHT_DECAY * master
-        mo[0] = mom
-        vo[0] = var
-        uo[0] = upd
-        for i, val in enumerate((master, upd)):
-            folded = jnp.sum((val * val).reshape(-1, 8, val.shape[-1]), axis=0)
-            lanes = folded[:, 0:128]
-            for j in range(1, val.shape[-1] // 128):
-                lanes = lanes + folded[:, j * 128:(j + 1) * 128]
-            sq[0, kind * 2 + i] += lanes
-
-    part(0, g1, a1, w1, m1, v1, m1o, v1o, u1o)
-    part(1, g2, a2, w2, m2, v2, m2o, v2o, u2o)
-
-
-def run_moments(g1, a1, w1, m1, v1, g2, a2, w2, m2, v2):
+    )(*args)
+
+
+def finalize_kernel(tot, g1, a1, w1, m1, v1, g2, a2, w2, m2, v2, w1o, m1o, v1o, w2o, m2o, v2o):
+    def part(kind, g, acc, w, m, v, wo, mo, vo):
+        scale = LEARN_RATE * jnp.sqrt(tot[0, 2 * kind:2 * kind + 1, 0:1] / tot[0, 2 * kind + 1:2 * kind + 2, 0:1])
+        mo[0], vo[0], upd = moments(g[0], acc[0], w[0], m[0], v[0])
+        wo[0] = w[0] - scale * upd
+
+    part(0, g1, a1, w1, m1, v1, w1o, m1o, v1o)
+    part(1, g2, a2, w2, m2, v2, w2o, m2o, v2o)
+
+
+def run_finalize(*args):
     up = pl.BlockSpec((1, 96, 768), lambda l, j: (l, 0, j))
     down = pl.BlockSpec((1, 96, 768), lambda l, j: (l, j, 0))
     s1 = jax.ShapeDtypeStruct((2, 96, FF), F32)
     s2 = jax.ShapeDtypeStruct((2, 384, D), F32)
     return pl.pallas_call(
-        moments_kernel,
+        finalize_kernel,
         grid=(2, 4),
-        out_shape=(s1, s1, s1, s2, s2, s2, jax.ShapeDtypeStruct((2, 4, 8, 128), F32)),
-        in_specs=[up] * 5 + [down] * 5,
-        out_specs=(up, up, up, down, down, down, pl.BlockSpec((1, 4, 8, 128), lambda l, j: (l, 0, 0, 0))),
-        name='moments',
-    )(g1, a1, w1, m1, v1, g2, a2, w2, m2, v2)
-
-
-def sums_kernel(sq_ref, out_ref, mine, got, snd, rcv):
-    me = position()[0]
-    mine[...] = jnp.sum(sq_ref[...], axis=1)
-    others = [lax.rem(me + i, 8) for i in range(1, 8)]
-    entry_barrier(others)
-    copies = []
-    for i, dev in enumerate(others):
-        copies.append(pltpu.make_async_remote_copy(src_ref=mine, dst_ref=got.at[i], send_sem=snd.at[i], recv_sem=rcv.at[i], device_id=(dev,), device_id_type=MESH))
-        copies[-1].start()
-    got[7] = mine[...]
-    for cp in copies:
-        cp.wait()
-    total = got[lax.rem(me + 7, 8)]
-    for dev in range(1, 8):
-        total = total + got[lax.rem(me + 7 - dev + 8, 8)]
-    out_ref[...] = jnp.broadcast_to(jnp.sum(total, axis=1, keepdims=True), (8, 128))
-
-
-def run_sums(sq):
-    vmem = pl.BlockSpec(memory_space=pltpu.VMEM)
-    return pl.pallas_call(
-        sums_kernel,
-        out_shape=jax.ShapeDtypeStruct((8, 128), F32),
-        in_specs=[vmem],
-        out_specs=vmem,
-        scratch_shapes=[pltpu.VMEM((8, 128), F32), pltpu.VMEM((8, 8, 128), F32), pltpu.SemaphoreType.DMA((7,)), pltpu.SemaphoreType.DMA((7,))],
-        compiler_params=pltpu.CompilerParams(collective_id=1, has_side_effects=True),
-        name='sums',
-    )(sq.reshape(8, 8, 128))
-
-
-def forward_kernel(w1_hbm, w2_hbm, x_hbm, o_ref, wf1, wf2, ab, xb, ld_sem, snd, rcv):
+        out_shape=(s1, s1, s1, s2, s2, s2),
+        in_specs=[pl.BlockSpec((1, 8, 128), lambda l, j: (l, 0, 0))] + [up] * 5 + [down] * 5,
+        out_specs=(up, up, up, down, down, down),
+        name='finalize',
+    )(*args)
+
+
+def forward_kernel(w1_hbm, w2_hbm, wg1_hbm, x_hbm, o_ref, wf1, wf2, ab, xb, ld_sem, snd, rcv):
     me, y, x, c, partner, xn, yn = position()
-    fulls = (wf1.at[0], wf2.at[0], wf1.at[1], wf2.at[1])
-    halves = (48, 192, 48, 192)
-    srcs = (w1_hbm.at[0], w2_hbm.at[0], w1_hbm.at[1], w2_hbm.at[1])
-    loads = [pltpu.make_async_copy(srcs[m], fulls[m].at[y, x, c], ld_sem.at[m]) for m in range(4)]
-    loads.append(pltpu.make_async_copy(x_hbm, xb, ld_sem.at[4]))
+    fulls = (wf1.at[0], wf2.at[0], wf2.at[1])
+    halves = (48, 192, 192)
+    srcs = (w1_hbm.at[0], w2_hbm.at[0], w2_hbm.at[1])
+    loads = [pltpu.make_async_copy(srcs[m], fulls[m].at[y, x, c], ld_sem.at[m]) for m in range(3)]
+    loads.append(pltpu.make_async_copy(x_hbm, xb, ld_sem.at[3]))
+    loads.append(pltpu.make_async_copy(wg1_hbm, wf1.at[1], ld_sem.at[4]))
     for cp in loads:
         cp.start()
     entry_barrier((partner, xn, yn))
@@ -416,49 +523,42 @@
                 fn()
         return hook
 
-    def second_and_next(m):
-        def fn():
-            second(m)
-            if m < 3:
-                first(m + 1)
-        return fn
-
     loads[0].wait()
     first(0)
-    for cp in loads[1:]:
+    for cp in loads[1:3]:
         cp.wait()
-    second_and_next(0)()
+    second(0)
+    first(1)
     third(0)
-    second_and_next(1)()
+    second(1)
+    first(2)
+    loads[3].wait()
+    loads[4].wait()
     done(0)
     up(0, no_hook)
     third(1)
     done(1)
-    down(0, at_step(3, second_and_next(2)))
-    third(2)
-    second_and_next(3)()
+    down(0, at_step(1, lambda: second(2)))
+    up(1, at_step(4, lambda: third(2)))
     done(2)
-    up(1, no_hook)
-    third(3)
-    done(3)
     down(1, no_hook)
 
 
-def run_forward(w1, w2, x):
+def run_forward(*args):
     any_spec = pl.BlockSpec(memory_space=pl.ANY)
     vm = pltpu.VMEM
     return pl.pallas_call(
         forward_kernel,
         out_shape=jax.ShapeDtypeStruct((TOK, D), BF16),
-        in_specs=[any_spec] * 3,
+        in_specs=[any_spec] * 4,
         out_specs=pl.BlockSpec(memory_space=vm),
         scratch_shapes=[
             vm((2, 2, 2, 2, 96, FF), BF16), vm((2, 2, 2, 2, 384, D), BF16), vm((TOK, FF), BF16), vm((TOK, D), BF16),
-            pltpu.SemaphoreType.DMA((5,)), pltpu.SemaphoreType.DMA((4, 9)), pltpu.SemaphoreType.DMA((4, 9)),
+            pltpu.SemaphoreType.DMA((5,)), pltpu.SemaphoreType.DMA((3, 9)), pltpu.SemaphoreType.DMA((3, 9)),
         ],
-        compiler_params=pltpu.CompilerParams(collective_id=2, has_side_effects=True, vmem_limit_bytes=VMEM_MAX),
+        compiler_params=pltpu.CompilerParams(collective_id=1, has_side_effects=True, vmem_limit_bytes=VMEM_MAX),
         name='forward',
-    )(w1, w2, x)
+    )(*args)
 
 
 def solution(mesh):
@@ -467,13 +567,9 @@
     spec_whole = P()
 
     def local_step(x_layers, dy_top, x_next, w_up, w_down, acc_up, acc_down, master_up, master_down, mom_up, mom_down, var_up, var_down):
-        g1, g2 = run_backward(x_layers.reshape(2, TOK, D), dy_top.reshape(TOK, D), w_up, w_down)
-        m1, v1, u1, m2, v2, u2, sq = run_moments(g1, acc_up, master_up, mom_up, var_up, g2, acc_down, master_down, mom_down, var_down)
-        tot = run_sums(sq)[:, 0].reshape(2, 4)
-        ratio = LEARN_RATE * jnp.sqrt(tot[:, 0::2] / tot[:, 1::2])
-        up_new = master_up - ratio[:, 0][:, None, None] * u1
-        down_new = master_down - ratio[:, 1][:, None, None] * u2
-        out = run_forward(up_new.astype(BF16), down_new.astype(BF16), x_next.reshape(TOK, D))
+        g1, g2, tot, ws1, ws2, wg1 = run_backward(x_layers.reshape(2, TOK, D), dy_top.reshape(TOK, D), w_up, w_down, acc_up, acc_down, master_up, master_down, mom_up, mom_down, var_up, var_down)
+        out = run_forward(ws1, ws2, wg1, x_next.reshape(TOK, D))
+        up_new, m1, v1, down_new, m2, v2 = run_finalize(tot, g1, acc_up, master_up, mom_up, var_up, g2, acc_down, master_down, mom_down, var_down)
         return up_new, down_new, m1, m2, v1, v2, out.reshape(1, TOK, D)
 
     return jax.shard_map(local_step, mesh=mesh, in_specs=(shard_rows, shard_batch, shard_batch, spec_whole, spec_whole) + (shard_rows,) * 8, out_specs=(shard_rows,) * 6 + (shard_batch,), check_vma=False)

time: 292 us -> 280 us (0.959)
  other arithmetic: 6.3 us -> 0 us
  local copies, waits for them, and re-layouts: 5.03 us -> 1.67 us
    pallas_call x1, Pallas kernels: 155 us -> 173 us  [run_backward(): pl.pallas_call(backward_kernel, out_shape=(jax.ShapeDtypeStruct((2, 96, F...]
    pallas_call x1, Pallas kernels: 104 us -> 88.4 us  [run_forward(): pl.pallas_call(forward_kernel, out_shape=jax.ShapeDtypeStruct((TOK, D), B...]
    convert_element_type x2 -> x0, other arithmetic: 6.28 us -> none  [the longest x1 4.02 us: local_step(): down_new.astype(BF16)]
    pallas_call x2 -> x1, Pallas kernels: 21.1 us -> 16.1 us  [run_finalize(): pl.pallas_call(finalize_kernel, grid=(2, 4), out_shape=(s1, s1, s1, s2, s...]
where the time goes in v2:
time: 280 us
  Pallas kernels  278 us (99%)
    pallas_call x1, Pallas kernels, run_backward(): pl.pallas_call(backward_kernel, out_shape=(jax.ShapeDtypeStruct((2, 96, F...  173 us
    pallas_call x1, Pallas kernels, run_forward(): pl.pallas_call(forward_kernel, out_shape=jax.ShapeDtypeStruct((TOK, D), B...  88.4 us
    pallas_call x1, Pallas kernels, run_finalize(): pl.pallas_call(finalize_kernel, grid=(2, 4), out_shape=(s1, s1, s1, s2, s...  16.1 us

profile of v2, /device:TPU:0, one launch (start us, length us, event | category | flops | bytes accessed | tf_op | source)
XLA Modules:
  0.0 279.9 jit_solution(7131752163189970113)
XLA Ops:
  0.6 173.0 %backward.1 = (f32[2,96,3072]{2,1,0:T(8,128)}, f32[2,384,768]{2,1,0:T(8,128)}, f32[2,8,128]{2,1,0:T(8,128)}, bf16[2,96,3072]{2,1,0:T(8,128)(2,1)}, bf16[2,384,76...) custom-call(bf16[2,2048,768]{2,1,0:T(8,128)(2,1)} %bitcast.5, bf16[2048,768]{1,0:T(8,128)(2,1)} %bitcast.6, ...), custom_call_target="tpu_custom_call" | custom-call | tf_op jit(solution)/shard_map/backward/pallas_call | solution.py:392
  173.7 88.4 %forward.1 = bf16[2048,768]{1,0:T(8,128)(2,1)} custom-call(bf16[2,96,3072]{2,1,0:T(8,128)(2,1)} %get-tuple-element.28.w1_hbm, bf16[2,384,768]{2,1,0:T(8,128)(2,1)} %get-tuple-element.29.w2_hbm, bf16[2,2,2,96,3072]{4,3,2,1,0:T(8,128)(2,1)} %get-tuple-element.30.wg1_hbm, bf16[2048,768]{1,0:T(8,128)(2,1)} %bitcast.7), custom_call_target="tpu_custom_call" | custom-call | tf_op jit(solution)/shard_map/forward/pallas_call | solution.py:550
  262.1 0.0 copy-start
  262.1 16.1 %finalize.1 = (f32[2,96,3072]{2,1,0:T(8,128)}, f32[2,96,3072]{2,1,0:T(8,128)}, f32[2,96,3072]{2,1,0:T(8,128)}, f32[2,384,768]{2,1,0:T(8,128)}, f32[2,384,768]{2,1,0:T(8,128)}, /*index=5*/f32[2,384,768]{2,1,0:T(8,128)}) custom-call(f32[2,8,128]{2,1,0:T(8,128)} %get-tuple-element.19.tot, f32[2,96,3072]{2,1,0:T(8,128)} %get-tuple-element.20.g1, ...), custom_call_target="tpu_custom_call" | custom-call | tf_op jit(solution)/shard_map/finalize/pallas_call | solution.py:431
  278.2 0.0 copy-done
  278.2 1.7 copy.21
Async XLA Ops:
  262.1 16.1 %copy-start = (bf16[2048,768]{1,0:T(8,128)(2,1)S(1)}, bf16[2048,768]{1,0:T(8,128)(2,1)}, u32[]{:S(2)}) copy-start(bf16[2048,768]{1,0:T(8,128)(2,1)} %forward.1) | copy-start | bytes 9437188

commit v3 on v0

v3 whole, which is shorter than its diff:
```python
import functools

import jax
import jax.numpy as jnp
from jax import lax
from jax.experimental import pallas as pl
from jax.experimental.pallas import tpu as pltpu
from jax.sharding import PartitionSpec as P

MICRO_STEPS = 2
STEP_COUNT = 3
BETA_MOM = 0.9
BETA_VAR = 0.999
ADAM_EPS = 1e-6
WEIGHT_DECAY = 0.01
LEARN_RATE = 0.06

C0 = 0.7978845608028654
C1 = C0 * 0.044715
MESH = pl.DeviceIdType.MESH
BF16 = jnp.bfloat16
F32 = jnp.float32
VMEM_MAX = 67043328

TOK = 2048
D = 768
FF = 3072
SUB = 128
CH = 8 * SUB
TT = 256
NT_DIMS = (((1,), (1,)), ((), ()))
NN_DIMS = (((1,), (0,)), ((), ()))


def position():
    me = lax.axis_index('fsdp')
    y, x, c = me // 4, (me // 2) % 2, me % 2
    return me, y, x, c, me + 1 - 2 * c, me + 2 - 4 * x, me + 4 - 8 * y


def entry_barrier(targets):
    barrier = pltpu.get_barrier_semaphore()
    for dev in targets:
        pl.semaphore_signal(barrier, inc=1, device_id=(dev,), device_id_type=MESH)
    pl.semaphore_wait(barrier, len(targets))


def dot(a, b, dims=NN_DIMS):
    return lax.dot_general(a, b, dims, preferred_element_type=F32)


def moments(grad_sum, acc, master, mom_prev, var_prev):
    grad = (acc + grad_sum) / MICRO_STEPS
    mom = BETA_MOM * mom_prev + (1.0 - BETA_MOM) * grad
    var = BETA_VAR * var_prev + (1.0 - BETA_VAR) * grad * grad
    upd = (mom / (1.0 - BETA_MOM ** STEP_COUNT)) / (jnp.sqrt(var / (1.0 - BETA_VAR ** STEP_COUNT)) + ADAM_EPS) + WEIGHT_DECAY * master
    return mom, var, upd


def step_kernel(x_hbm, dy_hbm, xn_hbm, w1_hbm, w2_hbm, acc1, acc2, mas1, mas2, mom1, mom2, var1, var2,
                wo1, wo2, mo1, mo2, vo1, vo2, out, wg1, wg2,
                xb, dyb, xt, dxacc, w1b, w2b, at, dhb, p1, p2, r01, r02, r1a1, r1b1, r1a2, r1b2, r2a1, r2b1, r2a2, r2b2,
                g1, g2, mb, sqb, smine, sgot, tot, ws1, ws2,
                ld_sem, w_sem, snd, rcv, l_sem, o_sem, x_snd, x_rcv, a_snd, a_rcv, b_snd, b_rcv, f_sem, out_sem):
    me, y, x, c, partner, xn, yn = position()
    others = [lax.rem(me + i, 8) for i in range(1, 8)]

    def column(q, cc, k):
        return pl.ds(pl.multiple_of((2 * q + cc) * 384 + k * SUB, SUB), SUB)

    def w_copies(g):
        layer = 1 - g // 3
        k = g % 3
        res = []
        for cc in range(2):
            for q in range(4):
                i = cc * 4 + q
                res.append(pltpu.make_async_copy(w1_hbm.at[layer, :, :, :, :, column(q, cc, k)], w1b.at[k, :, :, :, :, pl.ds(i * SUB, SUB)], w_sem.at[k, i]))
            res.append(pltpu.make_async_copy(w2_hbm.at[layer, :, :, cc, k], w2b.at[k, cc], w_sem.at[k, 8 + cc]))
        return res

    loads = [pltpu.make_async_copy(x_hbm.at[1], xb.at[1], ld_sem.at[0]),
             pltpu.make_async_copy(dy_hbm, dyb, ld_sem.at[1]),
             pltpu.make_async_copy(x_hbm.at[0], xb.at[0], ld_sem.at[2]),
             pltpu.make_async_copy(xn_hbm, xb.at[1], ld_sem.at[3])]
    for cp in loads[:2]:
        cp.start()
    for cp in w_copies(0):
        cp.start()
    loads[2].start()

    sqb[...] = jnp.zeros_like(sqb)
    smine[...] = jnp.zeros_like(smine)
    entry_barrier(others)

    def area(a, kind, j):
        return pl.ds(pl.multiple_of(a * 768 + j * 96, 96), 96) if kind == 0 else pl.ds(pl.multiple_of(a * 768 + 384 + j * SUB, SUB), SUB)

    def shard_pairs(up, down, layer, buf, a):
        res = [(up.at[layer, :, pl.ds(j * 768, 768)], buf.at[pl.ds(a * 768 + j * 96, 96), :]) for j in range(4)]
        res.append((down.at[layer], buf.at[pl.ds(a * 768 + 384, 384), :]))
        return res

    def lamb_loads(layer):
        res = []
        for a, (up, down) in enumerate(((acc1, acc2), (mom1, mom2), (var1, var2), (mas1, mas2))):
            for i, (src, dst) in enumerate(shard_pairs(up, down, layer, dxacc if a < 3 else mb, a % 3)):
                res.append(pltpu.make_async_copy(src, dst, l_sem.at[a, i]))
        return res

    def lamb_outs(layer, kinds, arrays):
        res = []
        for a, (up, down) in ((0, (wo1, wo2)), (1, (mo1, mo2)), (2, (vo1, vo2))):
            for i, (dst, src) in enumerate(shard_pairs(up, down, layer, mb if a == 0 else dxacc, a)):
                if a in arrays and i // 4 in kinds:
                    res.append(pltpu.make_async_copy(src, dst, o_sem.at[a, i]))
        return res

    def run(copies):
        for cp in copies:
            cp.start()

    def settle(copies):
        for cp in copies:
            cp.wait()

    def lamb_moments(layer, kind):
        @pl.loop(0, 4 - kind)
        def _(j):
            spans = [area(a, kind, j) for a in range(3)]
            grad_sum = g1[:, pl.ds(pl.multiple_of(j * 768, 768), 768)] if kind == 0 else g2[pl.ds(pl.multiple_of(j * SUB, SUB), SUB), :]
            master = mb[spans[0], :]
            mom, var, upd = moments(grad_sum, dxacc[spans[0], :], master, dxacc[spans[1], :], dxacc[spans[2], :])
            dxacc[spans[0], :] = upd
            dxacc[spans[1], :] = mom
            dxacc[spans[2], :] = var
            for i, val in enumerate((master, upd)):
                folded = jnp.sum((val * val).reshape(-1, 8, 768), axis=0)
                lanes = folded[:, 0:128]
                for b in range(1, 6):
                    lanes = lanes + folded[:, b * 128:(b + 1) * 128]
                sqb[layer, kind, i] += lanes

        for i in range(2):
            smine[layer, kind, i:i + 1, :] = jnp.sum(sqb[layer, kind, i], axis=0, keepdims=True)
        run(sum_copies(layer, kind))
        run(lamb_outs(layer, (kind,), (1, 2)))

    def sum_copies(layer, kind):
        return [pltpu.make_async_remote_copy(src_ref=smine.at[layer, kind], dst_ref=sgot.at[layer, kind, i], send_sem=x_snd.at[layer, kind, i], recv_sem=x_rcv.at[layer, kind, i], device_id=(dev,), device_id_type=MESH) for i, dev in enumerate(others)]

    def lamb_apply(layer, kind):
        sgot[layer, kind, 7] = smine[layer, kind]
        settle(sum_copies(layer, kind))
        total = sgot[layer, kind, lax.rem(me + 7, 8)]
        for dev in range(1, 8):
            total = total + sgot[layer, kind, lax.rem(me + 7 - dev + 8, 8)]
        tot[...] = jnp.broadcast_to(jnp.sum(total, axis=1, keepdims=True), (8, 128))
        scale = LEARN_RATE * jnp.sqrt(tot[0:1, 0:1] / tot[1:2, 0:1])

        @pl.loop(0, 4 - kind)
        def _(j):
            span = area(0, kind, j)
            new = mb[span, :] - scale * dxacc[span, :]
            mb[span, :] = new
            half = new.astype(BF16)
            if kind == 1:
                if layer == 1:
                    ws2[j] = half
                else:
                    w2b[j, c, y, x] = half
            else:
                for cc in range(2):
                    lanes = pl.ds(pl.multiple_of((cc * 4 + j) * SUB, SUB), SUB)
                    for k in range(3):
                        piece = half[:, cc * 384 + k * SUB:cc * 384 + (k + 1) * SUB]
                        if layer == 1:
                            ws1[k, :, lanes] = piece
                        else:
                            w1b[k, y, x, c, :, lanes] = piece

        run(lamb_outs(layer, (kind,), (0,)))

    def remote_copy(src, dst, s_sem, r_sem, dev):
        return pltpu.make_async_remote_copy(src_ref=src, dst_ref=dst, send_sem=s_sem, recv_sem=r_sem, device_id=(dev,), device_id_type=MESH)

    lo, hi = pl.ds(0, 48), pl.ds(48, 48)

    def gather_local():
        return pltpu.make_async_copy(ws1, wg1.at[:, y, x, c], ld_sem.at[4])

    def gather2_local():
        return pltpu.make_async_copy(ws2, wg2.at[:, c, y, x], ld_sem.at[5])

    def gather_parts(name):
        def go(src, dst, i, dev):
            return remote_copy(src, dst, a_snd.at[i], a_rcv.at[i], dev)
        if name == 's1':
            return (go(ws1.at[:, lo], wg1.at[:, y, x, c, lo], 0, xn), go(ws1.at[:, hi], wg1.at[:, y, x, c, hi], 1, yn))
        if name == 's2':
            return go(wg1.at[:, y, :, c, lo], wg1.at[:, y, :, c, lo], 2, yn), go(wg1.at[:, :, x, c, hi], wg1.at[:, :, x, c, hi], 3, xn)
        if name == 'd1':
            return (go(ws1, wg1.at[:, y, x, c], 4, partner),)
        if name == 'd2':
            return (go(wg1.at[:, y, 1 - x, c, lo], wg1.at[:, y, 1 - x, c, lo], 5, partner), go(wg1.at[:, 1 - y, x, c, hi], wg1.at[:, 1 - y, x, c, hi], 6, partner))
        return (go(wg1.at[:, 1 - y, :, c, lo], wg1.at[:, 1 - y, :, c, lo], 7, partner), go(wg1.at[:, :, 1 - x, c, hi], wg1.at[:, :, 1 - x, c, hi], 8, partner))

    def gather_start(*names):
        for name in names:
            run(gather_parts(name))

    def gather_wait(*names):
        for name in names:
            settle(gather_parts(name))

    def piece_parts(m, name):
        if m < 6 and m % 2 == 0:
            ref = w1b.at[m // 2]
            h = 48

            def blk(yy, xx, rows):
                return ref.at[yy, xx, c, rows]
        else:
            ref = w2b.at[m // 2] if m < 6 else wg2.at[m - 6]
            h = 64

            def blk(yy, xx, rows):
                return ref.at[c, yy, xx, rows]
        first, last, every, both = pl.ds(0, h), pl.ds(h, h), pl.ds(0, 2 * h), slice(None)

        def go(part, i, dev):
            return remote_copy(part, part, b_snd.at[m, i], b_rcv.at[m, i], dev)
        if name == 's1':
            return go(blk(y, x, first), 0, xn), go(blk(y, x, last), 1, yn)
        if name == 's2':
            return go(blk(y, both, first), 2, yn), go(blk(both, x, last), 3, xn)
        if name == 'd1':
            return (go(blk(y, x, every), 4, partner),)
        if name == 'd2':
            return go(blk(y, 1 - x, first), 5, partner), go(blk(1 - y, x, last), 6, partner)
        return go(blk(1 - y, both, first), 7, partner), go(blk(both, 1 - x, last), 8, partner)

    def first(m):
        run(piece_parts(m, 's1'))
        run(piece_parts(m, 'd1'))

    def second(m):
        settle(piece_parts(m, 's1'))
        run(piece_parts(m, 's2'))
        run(piece_parts(m, 'd2'))

    def third(m):
        settle(piece_parts(m, 's2'))
        run(piece_parts(m, 'd3'))

    def done(m):
        for name in ('d1', 'd2', 'd3'):
            settle(piece_parts(m, name))

    units = ((p1, r01, r1a1, r1b1, r2a1, r2b1, 48), (p2, r02, r1a2, r1b2, r2a2, r2b2, 64))

    def remote(src, dst, u, slot, stage, dev):
        return pltpu.make_async_remote_copy(src_ref=src, dst_ref=dst, send_sem=snd.at[u, slot, stage], recv_sem=rcv.at[u, slot, stage], device_id=(dev,), device_id_type=MESH)

    def s0(u, slot):
        p, r0, r1a, r1b, r2a, r2b, hr = units[u]
        return remote(p.at[slot, 1 - c], r0.at[slot], u, slot, 0, partner)

    def s1(u, slot):
        p, r0, r1a, r1b, r2a, r2b, hr = units[u]
        return (remote(p.at[slot, c, :, 1 - x, pl.ds(0, hr)], r1a.at[slot], u, slot, 1, xn),
                remote(p.at[slot, c, 1 - y, :, pl.ds(hr, hr)], r1b.at[slot], u, slot, 2, yn))

    def s2(u, slot):
        p, r0, r1a, r1b, r2a, r2b, hr = units[u]
        return (remote(p.at[slot, c, 1 - y, x, pl.ds(0, hr)], r2a.at[slot], u, slot, 3, yn),
                remote(p.at[slot, c, y, 1 - x, pl.ds(hr, hr)], r2b.at[slot], u, slot, 4, xn))

    def start_s0(u, slot):
        s0(u, slot).start()

    def to_s1(u, slot):
        p, r0, r1a, r1b, r2a, r2b, hr = units[u]
        s0(u, slot).wait()

        @pl.loop(0, 2)
        def _(yy):
            for xx in range(2):
                p[slot, c, yy, xx] = (p[slot, c, yy, xx].astype(F32) + r0[slot, yy, xx].astype(F32)).astype(BF16)

        for cp in s1(u, slot):
            cp.start()

    def to_s2(u, slot):
        p, r0, r1a, r1b, r2a, r2b, hr = units[u]
        ca, cb = s1(u, slot)
        ca.wait()
        for i in range(2):
            p[slot, c, i, x, 0:hr] = (p[slot, c, i, x, 0:hr].astype(F32) + r1a[slot, i].astype(F32)).astype(BF16)
        cb.wait()
        for i in range(2):
            p[slot, c, y, i, hr:2 * hr] = (p[slot, c, y, i, hr:2 * hr].astype(F32) + r1b[slot, i].astype(F32)).astype(BF16)
        for cp in s2(u, slot):
            cp.start()

    def finish(u, slot, g):
        p, r0, r1a, r1b, r2a, r2b, hr = units[u]
        k = g % 3
        ca, cb = s2(u, slot)
        for half, (cp, r2) in enumerate(((ca, r2a), (cb, r2b))):
            cp.wait()
            rows = slice(half * hr, half * hr + hr)
            total = p[slot, c, y, x, rows].astype(F32) + r2[slot].astype(F32)
            if u == 1:
                g2[pl.ds(pl.multiple_of(k * SUB + half * hr, 64), hr), :] = total
            else:
                for cc in range(2):
                    for q in range(4):
                        i = cc * 4 + q
                        g1[rows, column(q, cc, k)] = total[:, i * SUB:(i + 1) * SUB]

    settle(loads[:2])

    @pl.loop(0, 6)
    def _(g):
        slot = g % 2
        prev = 1 - slot
        layer = 1 - g // 3
        k = g % 3
        settle(w_copies(g))

        @pl.when(g < 5)
        def _():
            run(w_copies(g + 1))

        @pl.when(g == 3)
        def _():
            loads[2].wait()
            loads[3].start()
            run(lamb_loads(1))

        @pl.when(g == 5)
        def _():
            settle(lamb_outs(1, (0, 1), (0, 1, 2)))
            run(lamb_loads(0))

        def tile(rows):
            xv = xb[layer, rows, :]
            dyv = dyb[rows, :]
            xt[:, rows] = xv.T
            for n in range(CH // 256):
                cs = slice(n * 256, n * 256 + 256)
                h = dot(xv, w1b[k, :, :, :, :, cs].reshape(D, 256))
                da = dot(dyv, w2b[k, n // 2, n % 2].reshape(256, D), NT_DIMS)
                sq = h * h
                s = 0.5 * jnp.tanh(h * (C0 + C1 * sq)) + 0.5
                a = h * s
                gp = s + a * (1.0 - s) * (2.0 * C0 + (6.0 * C1) * sq)
                at[cs, rows] = a.astype(BF16).T
                dhb[rows, cs] = (da * gp).astype(BF16)

        def token_loop(with_dx):
            @pl.loop(0, TOK // (2 * TT))
            def _(t):
                @pl.when((g > 0) & (t == 1))
                def _():
                    to_s1(1, prev)

                if not with_dx:
                    @pl.when((g == 4) & (t == 2))
                    def _():
                        lamb_apply(1, 0)
                        gather_start('s1', 'd1')
                        gather_local().start()
                        lamb_apply(1, 1)
                        gather2_local().start()

                @pl.when((g > 0) & (t == 3))
                def _():
                    to_s2(0, prev)

                base = pl.multiple_of(t * (2 * TT), 2 * TT)
                spans = [pl.ds(base + i * TT, TT) for i in range(2)]
                for rows in spans:
                    tile(rows)
                if with_dx:
                    for rows in spans:
                        dxacc[rows, :] += dot(dhb[rows, :], w1b[k].reshape(D, CH), NT_DIMS)

        @pl.when(layer == 1)
        def _():
            @pl.when(k == 0)
            def _():
                @pl.loop(0, TOK // 128)
                def _(t):
                    rows = pl.ds(pl.multiple_of(t * 128, 128), 128)
                    dxacc[rows, :] = dyb[rows, :].astype(F32)

            token_loop(True)

        @pl.when(layer == 0)
        def _():
            token_loop(False)

        @pl.when(g > 0)
        def _():
            to_s2(1, prev)

        @pl.loop(0, CH // 256)
        def _(n):
            fs = pl.ds(pl.multiple_of(n * 256, 256), 256)
            res = dot(xt[...], dhb[:, fs]).astype(BF16)
            for b in range(8):
                p1[slot, b % 2, b // 4, (b // 2) % 2, :, fs] = res[b * 96:(b + 1) * 96]

        start_s0(0, slot)

        @pl.when(g > 0)
        def _():
            finish(0, prev, g - 1)

        @pl.loop(0, CH // 256)
        def _(n):
            fs = pl.ds(pl.multiple_of(n * 256, 256), 256)
            res = dot(at[fs, :], dyb[...]).astype(BF16)
            p2[slot, n // 2, n % 2] = res.reshape(2, SUB, D)

        to_s1(0, slot)
        start_s0(1, slot)

        @pl.when(g > 0)
        def _():
            finish(1, prev, g - 1)

        @pl.when(g == 2)
        def _():
            @pl.loop(0, TOK // TT)
            def _(t):
                rows = pl.ds(pl.multiple_of(t * TT, TT), TT)
                dyb[rows, :] = dxacc[rows, :].astype(BF16)

        @pl.when(g == 3)
        def _():
            settle(lamb_loads(1))
            lamb_moments(1, 0)
            lamb_moments(1, 1)

        @pl.when(g == 4)
        def _():
            gather_local().wait()
            gather_wait('s1')
            gather_start('s2', 'd2')

    to_s1(1, 1)
    to_s2(0, 1)
    to_s2(1, 1)
    settle(lamb_loads(0))
    finish(0, 1, 5)
    lamb_moments(0, 0)
    finish(1, 1, 5)
    lamb_moments(0, 1)
    lamb_apply(0, 0)
    first(0)
    first(2)
    lamb_apply(0, 1)
    second(0)
    first(1)
    second(2)
    first(3)
    second(1)
    first(4)
    gather_wait('s2')
    gather_start('d3')
    third(0)
    first(5)
    second(3)
    gather2_local().wait()
    loads[3].wait()
    settle(lamb_outs(0, (0, 1), (1, 2)))
    third(1)
    third(2)
    done(0)
    done(1)
    gather_wait('d1', 'd2', 'd3')

    def chunk_load(k, kind):
        if kind == 0:
            return pltpu.make_async_copy(wg1.at[k], w1b.at[k], f_sem.at[k, 0])
        return pltpu.make_async_copy(wg2.at[k], w2b.at[k], f_sem.at[k, 1])

    def out_copy(t):
        rows = pl.ds(pl.multiple_of(t * 512, 512), 512)
        return pltpu.make_async_copy(dyb.at[rows, :], out.at[rows, :], out_sem.at[t])

    def before_1():
        chunk_load(0, 0).start()
        second(5)
        first(6)
        first(7)
        third(3)
        done(2)
        done(3)

    def before_2():
        chunk_load(1, 0).start()
        third(5)
        done(4)
        done(5)

    def before_3():
        chunk_load(2, 0).start()
        second(8)
        done(6)
        chunk_load(0, 1).start()
        chunk_load(0, 0).wait()
        chunk_load(0, 1).wait()

    def before_4():
        chunk_load(1, 0).wait()
        chunk_load(1, 1).wait()

    def before_5():
        chunk_load(2, 0).wait()
        chunk_load(2, 1).wait()

    def load_second(m):
        done(m)
        chunk_load(m - 6, 1).start()

    def six_and_eight():
        second(6)
        first(8)

    hooks = {
        (0, 0): lambda: second(4),
        (1, 2): lambda: third(4),
        (1, 3): six_and_eight,
        (2, 1): lambda: second(7),
        (2, 3): lambda: third(6),
        (3, 1): lambda: third(7),
        (3, 3): lambda: load_second(7),
        (4, 1): lambda: third(8),
        (4, 3): lambda: load_second(8),
    }

    @pl.loop(0, 6)
    def _(f):
        k = f % 3
        for i, fn in enumerate((before_1, before_2, before_3, before_4, before_5)):
            pl.when(f == i + 1)(fn)

        @pl.when(k == 0)
        def _():
            @pl.loop(0, TOK // 128)
            def _(t):
                rows = pl.ds(pl.multiple_of(t * 128, 128), 128)
                dxacc[rows, :] = xb[1, rows, :].astype(F32)

        @pl.loop(0, TOK // (2 * TT))
        def _(t):
            for (hf, ht), fn in hooks.items():
                pl.when((f == hf) & (t == ht))(fn)
            base = pl.multiple_of(t * (2 * TT), 2 * TT)
            spans = [pl.ds(base + i * TT, TT) for i in range(2)]
            for rows in spans:
                xv = xb[1, rows, :]
                for n in range(CH // 256):
                    cs = slice(n * 256, n * 256 + 256)
                    h = dot(xv, w1b[k, :, :, :, :, cs].reshape(D, 256))
                    s = 0.5 * jnp.tanh(h * (C0 + C1 * (h * h))) + 0.5
                    dhb[rows, cs] = (h * s).astype(BF16)
            for rows in spans:
                dxacc[rows, :] += dot(dhb[rows, :], w2b[k].reshape(CH, D))

            pair = pl.ds(base, 2 * TT)

            @pl.when(f == 2)
            def _():
                xb[1, pair, :] = dxacc[pair, :].astype(BF16)

            @pl.when(f == 5)
            def _():
                dyb[pair, :] = dxacc[pair, :].astype(BF16)
                out_copy(t).start()

    settle(lamb_outs(0, (0, 1), (0,)))
    for t in range(4):
        out_copy(t).wait()


def run_step(*args):
    any_spec = pl.BlockSpec(memory_space=pl.ANY)
    vm = pltpu.VMEM
    dma = pltpu.SemaphoreType.DMA
    up, down = jax.ShapeDtypeStruct((2, 96, FF), F32), jax.ShapeDtypeStruct((2, 384, D), F32)
    return pl.pallas_call(
        step_kernel,
        out_shape=(up, down, up, down, up, down, jax.ShapeDtypeStruct((TOK, D), BF16),
                   jax.ShapeDtypeStruct((3, 2, 2, 2, 96, CH), BF16), jax.ShapeDtypeStruct((3, 2, 2, 2, SUB, D), BF16)),
        in_specs=[any_spec] * 13,
        out_specs=(any_spec,) * 9,
        scratch_shapes=[
            vm((2, TOK, D), BF16), vm((TOK, D), BF16), vm((D, TOK), BF16), vm((3 * 768, D), F32),
            vm((3, 2, 2, 2, 96, CH), BF16), vm((3, 2, 2, 2, SUB, D), BF16), vm((CH, TOK), BF16), vm((TOK, CH), BF16),
            vm((2, 2, 2, 2, 96, CH), BF16), vm((2, 2, 2, 2, SUB, D), BF16),
            vm((2, 2, 2, 96, CH), BF16), vm((2, 2, 2, SUB, D), BF16),
            vm((2, 2, 48, CH), BF16), vm((2, 2, 48, CH), BF16), vm((2, 2, 64, D), BF16), vm((2, 2, 64, D), BF16),
            vm((2, 48, CH), BF16), vm((2, 48, CH), BF16), vm((2, 64, D), BF16), vm((2, 64, D), BF16),
            vm((96, FF), F32), vm((384, D), F32), vm((768, 768), F32), vm((2, 2, 2, 8, 128), F32), vm((2, 2, 8, 128), F32), vm((2, 2, 8, 8, 128), F32), vm((8, 128), F32),
            vm((3, 96, CH), BF16), vm((3, SUB, D), BF16),
            dma((6,)), dma((3, 10)), dma((2, 2, 5)), dma((2, 2, 5)), dma((4, 5)), dma((3, 5)),
            dma((2, 2, 7)), dma((2, 2, 7)), dma((9,)), dma((9,)), dma((9, 9)), dma((9, 9)), dma((3, 2)), dma((4,)),
        ],
        compiler_params=pltpu.CompilerParams(collective_id=0, has_side_effects=True, vmem_limit_bytes=VMEM_MAX),
        name='step',
    )(*args)


def solution(mesh):
    shard_rows = P(None, 'fsdp')
    shard_batch = P('fsdp')
    spec_whole = P()

    def local_step(x_layers, dy_top, x_next, w_up, w_down, acc_up, acc_down, master_up, master_down, mom_up, mom_down, var_up, var_down):
        res = run_step(x_layers.reshape(2, TOK, D), dy_top.reshape(TOK, D), x_next.reshape(TOK, D),
                       w_up.reshape(2, 2, 2, 2, 96, FF), w_down.reshape(2, 2, 2, 2, 3, SUB, D),
                       acc_up, acc_down, master_up, master_down, mom_up, mom_down, var_up, var_down)
        return res[:6] + (res[6].reshape(1, TOK, D),)

    return jax.shard_map(local_step, mesh=mesh, in_specs=(shard_rows, shard_batch, shard_batch, spec_whole, spec_whole) + (shard_rows,) * 8, out_specs=(shard_rows,) * 6 + (shard_batch,), check_vma=False)
```

time: 495 us -> 280 us (0.57); the launches traced: 489 us -> 280 us
  Pallas kernels: 0 us -> 261 us
  matrix products: 229 us -> 0 us
  waiting for transfers between devices: 109 us -> 0 us
  other arithmetic: 48 us -> 0 us
  local copies, waits for them, and re-layouts: 59.9 us -> 17.9 us
  blocking collectives: 22.2 us -> 0 us
  between operations: 20.1 us -> 0.66 us
    pallas_call x0 -> x1, Pallas kernels: none -> 261 us  [run_step(): pl.pallas_call(step_kernel, out_shape=(up, down, up, down, up, down, jax....]
    dot_general x10 -> x0, matrix products: 229 us -> none  [the longest x2 55.6 us: layer_backward(): jnp.einsum('bsd,bsf->df', x_cur, d_pre, preferred_element_type=jnp.float32)]
    all_gather x4 -> x0, waiting for transfers between devices: 77 us -> none  [the longest x2 69.4 us: local_step(): lax.all_gather(up_new.astype(jnp.bfloat16), 'fsdp', axis=0, tiled=True)]
    unnamed x10 -> x0, waiting for transfers between devices: 31.5 us -> none
    unnamed x39 -> x19, local copies, waits for them, and re-layouts: 45.1 us -> 17.9 us
    psum x1 -> x0, blocking collectives: 22.2 us -> none  [local_step(): sq_total = lax.psum(sq_local, 'fsdp')]
    reduce_sum x4 -> x0, other arithmetic: 21.3 us -> none  [the longest x2 13.7 us: local_step(): jnp.sum(upd_up * upd_up)]
    another operation x6 -> x0, other arithmetic: 18.2 us -> none  [the longest x4 13 us: local_step(): jnp.stack([results[layer_id][field_id] for layer_id in range(layers)])]
  transfers between devices with their start and end apart: 8 -> 0, of which waited for: 5 -> 0; matrix products, arithmetic and copies ran while one was open for 46% -> 0% of each run, Pallas kernels for 0% -> 0%
where the time goes in v3:
time: 280 us
  Pallas kernels  261 us (93%)
  local copies, waits for them, and re-layouts  17.9 us (6%)
    pallas_call x1, Pallas kernels, run_step(): pl.pallas_call(step_kernel, out_shape=(up, down, up, down, up, down, jax....  261 us
    unnamed x19, local copies, waits for them, and re-layouts  17.9 us

profile of v3, /device:TPU:0, one launch (start us, length us, event | category | flops | bytes accessed | tf_op | source)
XLA Modules:
  0.0 279.9 jit_solution(12899815823138561728)
XLA Ops:
  0.6 261.3 %step.1 = (f32[2,96,3072]{2,1,0:T(8,128)}, f32[2,384,768]{2,1,0:T(8,128)}, f32[2,96,3072]{2,1,0:T(8,128)}, f32[2,384,768]{2,1,0:T(8,128)}, f32[2,96,3072]{2,1,0:...) custom-call(bf16[2,2048,768]{2,1,0:T(8,128)(2,1)} %bitcast.8, ...), custom_call_target="tpu_custom_call" | custom-call | tf_op jit(solution)/shard_map/step/pallas_call | solution.py:596
  262.0 0.0 copy-start.5
  262.0 3.4 %copy.27 = f32[2,96,3072]{2,1,0:T(8,128)} copy(f32[2,96,3072]{2,1,0:T(8,128)} %get-tuple-element.28) | data formatting | bytes 4718592
  265.4 0.0 copy-done.5
  265.4 0.0 copy-start.4
  265.4 1.4 copy.28
  266.8 1.1 copy-done.4
  268.0 0.0 copy-start.3
  268.0 1.4 copy.29
  269.4 1.1 copy-done.3
  270.5 0.0 copy-start.2
  270.5 1.4 copy.30
  271.9 1.1 copy-done.2
  273.0 0.0 copy-start.1
  273.0 1.4 copy.31
  274.4 1.1 copy-done.1
  275.5 0.0 copy-start
  275.5 1.4 copy.32
  276.9 1.3 copy-done
  278.3 1.7 copy.33
Async XLA Ops:
  262.0 3.5 %copy-start.5 = (f32[2,384,768]{2,1,0:T(8,128)S(1)}, f32[2,384,768]{2,1,0:T(8,128)}, u32[]{:S(2)}) copy-start(f32[2,384,768]{2,1,0:T(8,128)} %get-tuple-element.29) | copy-start | bytes 7077892
  265.4 2.5 copy-start.4
  268.0 2.5 copy-start.3
  270.5 2.5 copy-start.2
  273.0 2.5 copy-start.1
  275.5 2.7 copy-start

commit v4 on v3

--- a/solution.py
+++ b/solution.py
@@ -61,7 +61,7 @@
                 wo1, wo2, mo1, mo2, vo1, vo2, out, wg1, wg2,
                 xb, dyb, xt, dxacc, w1b, w2b, at, dhb, p1, p2, r01, r02, r1a1, r1b1, r1a2, r1b2, r2a1, r2b1, r2a2, r2b2,
                 g1, g2, mb, sqb, smine, sgot, tot, ws1, ws2,
-                ld_sem, w_sem, snd, rcv, l_sem, o_sem, x_snd, x_rcv, a_snd, a_rcv, b_snd, b_rcv, f_sem, out_sem):
+                ld_sem, w_sem, snd, rcv, l_sem, o_sem, x_snd, x_rcv, b_snd, b_rcv, f_sem, out_sem):
     me, y, x, c, partner, xn, yn = position()
     others = [lax.rem(me + i, 8) for i in range(1, 8)]
 
@@ -184,38 +184,15 @@
     def remote_copy(src, dst, s_sem, r_sem, dev):
         return pltpu.make_async_remote_copy(src_ref=src, dst_ref=dst, send_sem=s_sem, recv_sem=r_sem, device_id=(dev,), device_id_type=MESH)
 
-    lo, hi = pl.ds(0, 48), pl.ds(48, 48)
-
     def gather_local():
         return pltpu.make_async_copy(ws1, wg1.at[:, y, x, c], ld_sem.at[4])
 
     def gather2_local():
         return pltpu.make_async_copy(ws2, wg2.at[:, c, y, x], ld_sem.at[5])
 
-    def gather_parts(name):
-        def go(src, dst, i, dev):
-            return remote_copy(src, dst, a_snd.at[i], a_rcv.at[i], dev)
-        if name == 's1':
-            return (go(ws1.at[:, lo], wg1.at[:, y, x, c, lo], 0, xn), go(ws1.at[:, hi], wg1.at[:, y, x, c, hi], 1, yn))
-        if name == 's2':
-            return go(wg1.at[:, y, :, c, lo], wg1.at[:, y, :, c, lo], 2, yn), go(wg1.at[:, :, x, c, hi], wg1.at[:, :, x, c, hi], 3, xn)
-        if name == 'd1':
-            return (go(ws1, wg1.at[:, y, x, c], 4, partner),)
-        if name == 'd2':
-            return (go(wg1.at[:, y, 1 - x, c, lo], wg1.at[:, y, 1 - x, c, lo], 5, partner), go(wg1.at[:, 1 - y, x, c, hi], wg1.at[:, 1 - y, x, c, hi], 6, partner))
-        return (go(wg1.at[:, 1 - y, :, c, lo], wg1.at[:, 1 - y, :, c, lo], 7, partner), go(wg1.at[:, :, 1 - x, c, hi], wg1.at[:, :, 1 - x, c, hi], 8, partner))
-
-    def gather_start(*names):
-        for name in names:
-            run(gather_parts(name))
-
-    def gather_wait(*names):
-        for name in names:
-            settle(gather_parts(name))
-
     def piece_parts(m, name):
-        if m < 6 and m % 2 == 0:
-            ref = w1b.at[m // 2]
+        if m > 8 or (m < 6 and m % 2 == 0):
+            ref = w1b.at[m // 2] if m < 6 else wg1.at[m - 9]
             h = 48
 
             def blk(yy, xx, rows):
@@ -370,10 +347,13 @@
                     @pl.when((g == 4) & (t == 2))
                     def _():
                         lamb_apply(1, 0)
-                        gather_start('s1', 'd1')
                         gather_local().start()
                         lamb_apply(1, 1)
                         gather2_local().start()
+
+                    @pl.when((g == 5) & (t == 2))
+                    def _():
+                        second(9)
 
                 @pl.when((g > 0) & (t == 3))
                 def _():
@@ -406,6 +386,13 @@
         def _():
             to_s2(1, prev)
 
+        @pl.when(g == 4)
+        def _():
+            gather_local().wait()
+            gather2_local().wait()
+            for m in (9, 10, 11):
+                first(m)
+
         @pl.loop(0, CH // 256)
         def _(n):
             fs = pl.ds(pl.multiple_of(n * 256, 256), 256)
@@ -445,15 +432,10 @@
             lamb_moments(1, 0)
             lamb_moments(1, 1)
 
-        @pl.when(g == 4)
-        def _():
-            gather_local().wait()
-            gather_wait('s1')
-            gather_start('s2', 'd2')
-
     to_s1(1, 1)
     to_s2(0, 1)
     to_s2(1, 1)
+    first(6)
     settle(lamb_loads(0))
     finish(0, 1, 5)
     lamb_moments(0, 0)
@@ -461,27 +443,22 @@
     lamb_moments(0, 1)
     lamb_apply(0, 0)
     first(0)
+    lamb_apply(0, 1)
+    first(1)
+    second(0)
     first(2)
-    lamb_apply(0, 1)
-    second(0)
-    first(1)
+    second(1)
+    first(3)
+    first(4)
+    third(0)
     second(2)
-    first(3)
-    second(1)
-    first(4)
-    gather_wait('s2')
-    gather_start('d3')
-    third(0)
     first(5)
-    second(3)
-    gather2_local().wait()
+    third(9)
     loads[3].wait()
     settle(lamb_outs(0, (0, 1), (1, 2)))
     third(1)
-    third(2)
     done(0)
     done(1)
-    gather_wait('d1', 'd2', 'd3')
 
     def chunk_load(k, kind):
         if kind == 0:
@@ -492,55 +469,63 @@
         rows = pl.ds(pl.multiple_of(t * 512, 512), 512)
         return pltpu.make_async_copy(dyb.at[rows, :], out.at[rows, :], out_sem.at[t])
 
+    def load(k, kind):
+        done(9 + k if kind == 0 else 6 + k)
+        chunk_load(k, kind).start()
+
+    def ready(k):
+        chunk_load(k, 0).wait()
+        chunk_load(k, 1).wait()
+
     def before_1():
-        chunk_load(0, 0).start()
         second(5)
-        first(6)
         first(7)
         third(3)
         done(2)
         done(3)
+        load(0, 0)
 
     def before_2():
-        chunk_load(1, 0).start()
         third(5)
         done(4)
         done(5)
+        second(7)
+        first(8)
+        second(11)
 
     def before_3():
-        chunk_load(2, 0).start()
+        load(0, 1)
+        third(10)
+        ready(0)
+
+    def before_4():
+        third(11)
+        ready(1)
+
+    def before_5():
+        ready(2)
+
+    def f1_t1():
+        third(4)
+        second(6)
+
+    def f3_t3():
         second(8)
-        done(6)
-        chunk_load(0, 1).start()
-        chunk_load(0, 0).wait()
-        chunk_load(0, 1).wait()
-
-    def before_4():
-        chunk_load(1, 0).wait()
-        chunk_load(1, 1).wait()
-
-    def before_5():
-        chunk_load(2, 0).wait()
-        chunk_load(2, 1).wait()
-
-    def load_second(m):
-        done(m)
-        chunk_load(m - 6, 1).start()
-
-    def six_and_eight():
-        second(6)
-        first(8)
+        load(1, 1)
 
     hooks = {
-        (0, 0): lambda: second(4),
-        (1, 2): lambda: third(4),
-        (1, 3): six_and_eight,
-        (2, 1): lambda: second(7),
-        (2, 3): lambda: third(6),
+        (0, 0): lambda: second(3),
+        (0, 1): lambda: second(4),
+        (0, 3): lambda: third(2),
+        (1, 1): f1_t1,
+        (1, 2): lambda: second(10),
+        (2, 2): lambda: third(6),
         (3, 1): lambda: third(7),
-        (3, 3): lambda: load_second(7),
-        (4, 1): lambda: third(8),
-        (4, 3): lambda: load_second(8),
+        (3, 2): lambda: load(1, 0),
+        (3, 3): f3_t3,
+        (4, 1): lambda: load(2, 0),
+        (4, 2): lambda: third(8),
+        (4, 3): lambda: load(2, 1),
     }
 
     @pl.loop(0, 6)
@@ -609,13 +594,44 @@
             vm((96, FF), F32), vm((384, D), F32), vm((768, 768), F32), vm((2, 2, 2, 8, 128), F32), vm((2, 2, 8, 128), F32), vm((2, 2, 8, 8, 128), F32), vm((8, 128), F32),
             vm((3, 96, CH), BF16), vm((3, SUB, D), BF16),
             dma((6,)), dma((3, 10)), dma((2, 2, 5)), dma((2, 2, 5)), dma((4, 5)), dma((3, 5)),
-            dma((2, 2, 7)), dma((2, 2, 7)), dma((9,)), dma((9,)), dma((9, 9)), dma((9, 9)), dma((3, 2)), dma((4,)),
+            dma((2, 2, 7)), dma((2, 2, 7)), dma((12, 9)), dma((12, 9)), dma((3, 2)), dma((4,)),
         ],
         compiler_params=pltpu.CompilerParams(collective_id=0, has_side_effects=True, vmem_limit_bytes=VMEM_MAX),
         name='step',
     )(*args)
 
 
+def copy_kernel(*refs):
+    src, dst, buf, (sem_in, sem_out) = refs[:7], refs[7:14], refs[14:21], refs[21:]
+    order = [(a, i) for i in range(2) for a in range(7)]
+
+    def part(ref, a, i):
+        return ref.at[pl.ds(i * (TOK // 2), TOK // 2)] if a == 6 else ref.at[i]
+
+    ins = [pltpu.make_async_copy(part(src[a], a, i), part(buf[a], a, i), sem_in.at[a, i]) for a, i in order]
+    outs = [pltpu.make_async_copy(part(buf[a], a, i), part(dst[a], a, i), sem_out.at[a, i]) for a, i in order]
+    for cp in ins:
+        cp.start()
+    for cp, nxt in zip(ins, outs):
+        cp.wait()
+        nxt.start()
+    for cp in outs:
+        cp.wait()
+
+
+def run_copy(arrays):
+    any_spec = pl.BlockSpec(memory_space=pl.ANY)
+    return pl.pallas_call(
+        copy_kernel,
+        out_shape=tuple(jax.ShapeDtypeStruct(a.shape, a.dtype) for a in arrays),
+        in_specs=[any_spec] * 7,
+        out_specs=(any_spec,) * 7,
+        scratch_shapes=[pltpu.VMEM(a.shape, a.dtype) for a in arrays] + [pltpu.SemaphoreType.DMA((7, 2)), pltpu.SemaphoreType.DMA((7, 2))],
+        compiler_params=pltpu.CompilerParams(vmem_limit_bytes=VMEM_MAX),
+        name='copy_out',
+    )(*arrays)
+
+
 def solution(mesh):
     shard_rows = P(None, 'fsdp')
     shard_batch = P('fsdp')
@@ -625,6 +641,7 @@
         res = run_step(x_layers.reshape(2, TOK, D), dy_top.reshape(TOK, D), x_next.reshape(TOK, D),
                        w_up.reshape(2, 2, 2, 2, 96, FF), w_down.reshape(2, 2, 2, 2, 3, SUB, D),
                        acc_up, acc_down, master_up, master_down, mom_up, mom_down, var_up, var_down)
-        return res[:6] + (res[6].reshape(1, TOK, D),)
+        res = run_copy(res[:7])
+        return tuple(res[:6]) + (res[6].reshape(1, TOK, D),)
 
     return jax.shard_map(local_step, mesh=mesh, in_specs=(shard_rows, shard_batch, shard_batch, spec_whole, spec_whole) + (shard_rows,) * 8, out_specs=(shard_rows,) * 6 + (shard_batch,), check_vma=False)

time: 280 us -> 260 us (0.929)
  local copies, waits for them, and re-layouts: 17.9 us -> 0 us
    unnamed x19 -> x0, local copies, waits for them, and re-layouts: 17.9 us -> none
    pallas_call x1, Pallas kernels: 261 us -> 246 us  [run_step(): pl.pallas_call(step_kernel, out_shape=(up, down, up, down, up, down, jax....]
    pallas_call x0 -> x1, Pallas kernels: none -> 12.6 us  [run_copy(): pl.pallas_call(copy_kernel, out_shape=tuple((jax.ShapeDtypeStruct(a.shape...]
where the time goes in v4:
time: 260 us
  Pallas kernels  259 us (100%)
    pallas_call x1, Pallas kernels, run_step(): pl.pallas_call(step_kernel, out_shape=(up, down, up, down, up, down, jax....  246 us
    pallas_call x1, Pallas kernels, run_copy(): pl.pallas_call(copy_kernel, out_shape=tuple((jax.ShapeDtypeStruct(a.shape...  12.6 us

profile of v4, /device:TPU:0, one launch (start us, length us, event | category | flops | bytes accessed | tf_op | source)
XLA Modules:
  0.0 259.7 jit_solution(3396455930275969350)
XLA Ops:
  0.6 246.3 %step.1 = (f32[2,96,3072]{2,1,0:T(8,128)}, f32[2,384,768]{2,1,0:T(8,128)}, f32[2,96,3072]{2,1,0:T(8,128)}, f32[2,384,768]{2,1,0:T(8,128)}, f32[2,96,3072]{2,1,0:...) custom-call(bf16[2,2048,768]{2,1,0:T(8,128)(2,1)} %bitcast.8, ...), custom_call_target="tpu_custom_call" | custom-call | tf_op jit(solution)/shard_map/step/pallas_call | solution.py:581
  246.9 12.6 %copy_out.1 = (f32[2,96,3072]{2,1,0:T(8,128)}, f32[2,384,768]{2,1,0:T(8,128)}, f32[2,96,3072]{2,1,0:T(8,128)}, f32[2,384,768]{2,1,0:T(8,128)}, f32[2,96,3072]{2,...) custom-call(f32[2,96,3072]{2,1,0:T(8,128)} %get-tuple-element.21.refs_0_, ...), custom_call_target="tpu_custom_call" | custom-call | tf_op jit(solution)/shard_map/copy_out/pallas_call | solution.py:624

commit v5 on v4

--- a/solution.py
+++ b/solution.py
@@ -393,23 +393,16 @@
             for m in (9, 10, 11):
                 first(m)
 
-        @pl.loop(0, CH // 256)
-        def _(n):
-            fs = pl.ds(pl.multiple_of(n * 256, 256), 256)
+        for n in range(CH // 256):
+            fs = slice(n * 256, n * 256 + 256)
             res = dot(xt[...], dhb[:, fs]).astype(BF16)
             for b in range(8):
                 p1[slot, b % 2, b // 4, (b // 2) % 2, :, fs] = res[b * 96:(b + 1) * 96]
 
         start_s0(0, slot)
 
-        @pl.when(g > 0)
-        def _():
-            finish(0, prev, g - 1)
-
-        @pl.loop(0, CH // 256)
-        def _(n):
-            fs = pl.ds(pl.multiple_of(n * 256, 256), 256)
-            res = dot(at[fs, :], dyb[...]).astype(BF16)
+        for n in range(CH // 256):
+            res = dot(at[n * 256:n * 256 + 256, :], dyb[...]).astype(BF16)
             p2[slot, n // 2, n % 2] = res.reshape(2, SUB, D)
 
         to_s1(0, slot)
@@ -417,6 +410,7 @@
 
         @pl.when(g > 0)
         def _():
+            finish(0, prev, g - 1)
             finish(1, prev, g - 1)
 
         @pl.when(g == 2)

time: 260 us -> 252 us (0.969)
  Pallas kernels: 259 us -> 251 us
    pallas_call x1, Pallas kernels: 246 us -> 238 us  [run_step(): pl.pallas_call(step_kernel, out_shape=(up, down, up, down, up, down, jax....]
where the time goes in v5:
time: 252 us
  Pallas kernels  251 us (100%)
    pallas_call x1, Pallas kernels, run_step(): pl.pallas_call(step_kernel, out_shape=(up, down, up, down, up, down, jax....  238 us
    pallas_call x1, Pallas kernels, run_copy(): pl.pallas_call(copy_kernel, out_shape=tuple((jax.ShapeDtypeStruct(a.shape...  12.6 us

profile of v5, /device:TPU:0, one launch (start us, length us, event | category | flops | bytes accessed | tf_op | source)
XLA Modules:
  0.0 251.8 jit_solution(6141567873275143875)
XLA Ops:
  0.6 238.4 %step.1 = (f32[2,96,3072]{2,1,0:T(8,128)}, f32[2,384,768]{2,1,0:T(8,128)}, f32[2,96,3072]{2,1,0:T(8,128)}, f32[2,384,768]{2,1,0:T(8,128)}, f32[2,96,3072]{2,1,0:...) custom-call(bf16[2,2048,768]{2,1,0:T(8,128)(2,1)} %bitcast.8, ...), custom_call_target="tpu_custom_call" | custom-call | tf_op jit(solution)/shard_map/step/pallas_call | solution.py:575
  239.0 12.6 %copy_out.1 = (f32[2,96,3072]{2,1,0:T(8,128)}, f32[2,384,768]{2,1,0:T(8,128)}, f32[2,96,3072]{2,1,0:T(8,128)}, f32[2,384,768]{2,1,0:T(8,128)}, f32[2,96,3072]{2,...) custom-call(f32[2,96,3072]{2,1,0:T(8,128)} %get-tuple-element.21.refs_0_, ...), custom_call_target="tpu_custom_call" | custom-call | tf_op jit(solution)/shard_map/copy_out/pallas_call | solution.py:618

commit v6 on v5

--- a/solution.py
+++ b/solution.py
@@ -87,8 +87,6 @@
         cp.start()
     for cp in w_copies(0):
         cp.start()
-    loads[2].start()
-
     sqb[...] = jnp.zeros_like(sqb)
     smine[...] = jnp.zeros_like(smine)
     entry_barrier(others)
@@ -310,6 +308,10 @@
         def _():
             run(w_copies(g + 1))
 
+        @pl.when(g == 1)
+        def _():
+            loads[2].start()
+
         @pl.when(g == 3)
         def _():
             loads[2].wait()
@@ -337,30 +339,22 @@
                 dhb[rows, cs] = (da * gp).astype(BF16)
 
         def token_loop(with_dx):
-            @pl.loop(0, TOK // (2 * TT))
+            @pl.loop(0, TOK // (4 * TT))
             def _(t):
                 @pl.when((g > 0) & (t == 1))
                 def _():
                     to_s1(1, prev)
 
                 if not with_dx:
-                    @pl.when((g == 4) & (t == 2))
+                    @pl.when((g == 4) & (t == 1))
                     def _():
                         lamb_apply(1, 0)
                         gather_local().start()
                         lamb_apply(1, 1)
                         gather2_local().start()
 
-                    @pl.when((g == 5) & (t == 2))
-                    def _():
-                        second(9)
-
-                @pl.when((g > 0) & (t == 3))
-                def _():
-                    to_s2(0, prev)
-
-                base = pl.multiple_of(t * (2 * TT), 2 * TT)
-                spans = [pl.ds(base + i * TT, TT) for i in range(2)]
+                base = pl.multiple_of(t * (4 * TT), 4 * TT)
+                spans = [pl.ds(base + i * TT, TT) for i in range(4)]
                 for rows in spans:
                     tile(rows)
                 if with_dx:
@@ -384,7 +378,7 @@
 
         @pl.when(g > 0)
         def _():
-            to_s2(1, prev)
+            to_s2(0, prev)
 
         @pl.when(g == 4)
         def _():
@@ -394,6 +388,10 @@
                 first(m)
 
         for n in range(CH // 256):
+            if n == 2:
+                @pl.when(g > 0)
+                def _():
+                    to_s2(1, prev)
             fs = slice(n * 256, n * 256 + 256)
             res = dot(xt[...], dhb[:, fs]).astype(BF16)
             for b in range(8):
@@ -447,7 +445,6 @@
     third(0)
     second(2)
     first(5)
-    third(9)
     loads[3].wait()
     settle(lamb_outs(0, (0, 1), (1, 2)))
     third(1)
@@ -473,14 +470,15 @@
 
     def before_1():
         second(5)
+        second(9)
         first(7)
         third(3)
         done(2)
         done(3)
-        load(0, 0)
 
     def before_2():
         third(5)
+        third(9)
         done(4)
         done(5)
         second(7)
@@ -488,6 +486,7 @@
         second(11)
 
     def before_3():
+        load(0, 0)
         load(0, 1)
         third(10)
         ready(0)

time: 252 us -> 255 us (1.012)
  Pallas kernels: 251 us -> 254 us
    pallas_call x1, Pallas kernels: 238 us -> 241 us  [run_step(): pl.pallas_call(step_kernel, out_shape=(up, down, up, down, up, down, jax....]
where the time goes in v6:
time: 255 us
  Pallas kernels  254 us (100%)
    pallas_call x1, Pallas kernels, run_step(): pl.pallas_call(step_kernel, out_shape=(up, down, up, down, up, down, jax....  241 us
    pallas_call x1, Pallas kernels, run_copy(): pl.pallas_call(copy_kernel, out_shape=tuple((jax.ShapeDtypeStruct(a.shape...  12.6 us

profile of v6, /device:TPU:0, one launch (start us, length us, event | category | flops | bytes accessed | tf_op | source)
XLA Modules:
  0.0 254.8 jit_solution(8270502475673589268)
XLA Ops:
  0.6 241.4 %step.1 = (f32[2,96,3072]{2,1,0:T(8,128)}, f32[2,384,768]{2,1,0:T(8,128)}, f32[2,96,3072]{2,1,0:T(8,128)}, f32[2,384,768]{2,1,0:T(8,128)}, f32[2,96,3072]{2,1,0:...) custom-call(bf16[2,2048,768]{2,1,0:T(8,128)(2,1)} %bitcast.8, ...), custom_call_target="tpu_custom_call" | custom-call | tf_op jit(solution)/shard_map/step/pallas_call | solution.py:574
  242.1 12.6 %copy_out.1 = (f32[2,96,3072]{2,1,0:T(8,128)}, f32[2,384,768]{2,1,0:T(8,128)}, f32[2,96,3072]{2,1,0:T(8,128)}, f32[2,384,768]{2,1,0:T(8,128)}, f32[2,96,3072]{2,...) custom-call(f32[2,96,3072]{2,1,0:T(8,128)} %get-tuple-element.21.refs_0_, ...), custom_call_target="tpu_custom_call" | custom-call | tf_op jit(solution)/shard_map/copy_out/pallas_call | solution.py:617

commit v7 on v6

--- a/solution.py
+++ b/solution.py
@@ -346,6 +346,10 @@
                     to_s1(1, prev)
 
                 if not with_dx:
+                    @pl.when((g == 5) & (t == 1))
+                    def _():
+                        second(9)
+
                     @pl.when((g == 4) & (t == 1))
                     def _():
                         lamb_apply(1, 0)
@@ -380,18 +384,19 @@
         def _():
             to_s2(0, prev)
 
-        @pl.when(g == 4)
-        def _():
-            gather_local().wait()
-            gather2_local().wait()
-            for m in (9, 10, 11):
-                first(m)
-
         for n in range(CH // 256):
             if n == 2:
                 @pl.when(g > 0)
                 def _():
                     to_s2(1, prev)
+
+                @pl.when(g == 4)
+                def _():
+                    gather_local().wait()
+                    gather2_local().wait()
+                    for m in (9, 10, 11):
+                        first(m)
+
             fs = slice(n * 256, n * 256 + 256)
             res = dot(xt[...], dhb[:, fs]).astype(BF16)
             for b in range(8):
@@ -445,6 +450,7 @@
     third(0)
     second(2)
     first(5)
+    third(9)
     loads[3].wait()
     settle(lamb_outs(0, (0, 1), (1, 2)))
     third(1)
@@ -470,15 +476,14 @@
 
     def before_1():
         second(5)
-        second(9)
         first(7)
         third(3)
         done(2)
         done(3)
+        load(0, 0)
 
     def before_2():
         third(5)
-        third(9)
         done(4)
         done(5)
         second(7)
@@ -486,7 +491,6 @@
         second(11)
 
     def before_3():
-        load(0, 0)
         load(0, 1)
         third(10)
         ready(0)

time: 255 us -> 252 us (0.988)
  Pallas kernels: 254 us -> 251 us
    pallas_call x1, Pallas kernels: 241 us -> 238 us  [run_step(): pl.pallas_call(step_kernel, out_shape=(up, down, up, down, up, down, jax....]
where the time goes in v7:
time: 252 us; the launch traced here: 251 us
  Pallas kernels  251 us (100%)
    pallas_call x1, Pallas kernels, run_step(): pl.pallas_call(step_kernel, out_shape=(up, down, up, down, up, down, jax....  238 us
    pallas_call x1, Pallas kernels, run_copy(): pl.pallas_call(copy_kernel, out_shape=tuple((jax.ShapeDtypeStruct(a.shape...  12.6 us

profile of v7, /device:TPU:0, one launch (start us, length us, event | category | flops | bytes accessed | tf_op | source)
XLA Modules:
  0.0 251.4 jit_solution(5500820581279015219)
XLA Ops:
  0.6 238.0 %step.1 = (f32[2,96,3072]{2,1,0:T(8,128)}, f32[2,384,768]{2,1,0:T(8,128)}, f32[2,96,3072]{2,1,0:T(8,128)}, f32[2,384,768]{2,1,0:T(8,128)}, f32[2,96,3072]{2,1,0:...) custom-call(bf16[2,2048,768]{2,1,0:T(8,128)(2,1)} %bitcast.8, ...), custom_call_target="tpu_custom_call" | custom-call | tf_op jit(solution)/shard_map/step/pallas_call | solution.py:578
  238.6 12.6 %copy_out.1 = (f32[2,96,3072]{2,1,0:T(8,128)}, f32[2,384,768]{2,1,0:T(8,128)}, f32[2,96,3072]{2,1,0:T(8,128)}, f32[2,384,768]{2,1,0:T(8,128)}, f32[2,96,3072]{2,...) custom-call(f32[2,96,3072]{2,1,0:T(8,128)} %get-tuple-element.21.refs_0_, ...), custom_call_target="tpu_custom_call" | custom-call | tf_op jit(solution)/shard_map/copy_out/pallas_call | solution.py:621

commit v8 on v7

--- a/solution.py
+++ b/solution.py
@@ -188,7 +188,21 @@
     def gather2_local():
         return pltpu.make_async_copy(ws2, wg2.at[:, c, y, x], ld_sem.at[5])
 
+    groups = {0: 1, 1: 1, 2: 2, 3: 2, 6: 1, 7: 1, 8: 1, 9: 3}
+
     def piece_parts(m, name):
+        if name in ('s1', 'd1'):
+            if m not in groups:
+                return ()
+            span = pl.ds(m // 2 if m < 6 else m % 3, groups[m])
+            if m > 8 or (m < 6 and m % 2 == 0):
+                ref, h = (w1b if m < 6 else wg1).at[span, y, x, c], 48
+            else:
+                ref, h = (w2b if m < 6 else wg2).at[span, c, y, x], 64
+            if name == 'd1':
+                return (remote_copy(ref, ref, b_snd.at[m, 4], b_rcv.at[m, 4], partner),)
+            lower, upper = ref.at[:, pl.ds(0, h)], ref.at[:, pl.ds(h, h)]
+            return remote_copy(lower, lower, b_snd.at[m, 0], b_rcv.at[m, 0], xn), remote_copy(upper, upper, b_snd.at[m, 1], b_rcv.at[m, 1], yn)
         if m > 8 or (m < 6 and m % 2 == 0):
             ref = w1b.at[m // 2] if m < 6 else wg1.at[m - 9]
             h = 48
@@ -201,16 +215,12 @@
 
             def blk(yy, xx, rows):
                 return ref.at[c, yy, xx, rows]
-        first, last, every, both = pl.ds(0, h), pl.ds(h, h), pl.ds(0, 2 * h), slice(None)
+        first, last, both = pl.ds(0, h), pl.ds(h, h), slice(None)
 
         def go(part, i, dev):
             return remote_copy(part, part, b_snd.at[m, i], b_rcv.at[m, i], dev)
-        if name == 's1':
-            return go(blk(y, x, first), 0, xn), go(blk(y, x, last), 1, yn)
         if name == 's2':
             return go(blk(y, both, first), 2, yn), go(blk(both, x, last), 3, xn)
-        if name == 'd1':
-            return (go(blk(y, x, every), 4, partner),)
         if name == 'd2':
             return go(blk(y, 1 - x, first), 5, partner), go(blk(1 - y, x, last), 6, partner)
         return go(blk(1 - y, both, first), 7, partner), go(blk(both, 1 - x, last), 8, partner)
@@ -394,8 +404,7 @@
                 def _():
                     gather_local().wait()
                     gather2_local().wait()
-                    for m in (9, 10, 11):
-                        first(m)
+                    first(9)
 
             fs = slice(n * 256, n * 256 + 256)
             res = dot(xt[...], dhb[:, fs]).astype(BF16)
@@ -446,10 +455,8 @@
     first(2)
     second(1)
     first(3)
-    first(4)
     third(0)
     second(2)
-    first(5)
     third(9)
     loads[3].wait()
     settle(lamb_outs(0, (0, 1), (1, 2)))

time: 252 us -> 253 us (level)
  no operation moved by 1% of the time
where the time goes in v8:
time: 253 us
  Pallas kernels  252 us (100%)
    pallas_call x1, Pallas kernels, run_step(): pl.pallas_call(step_kernel, out_shape=(up, down, up, down, up, down, jax....  239 us
    pallas_call x1, Pallas kernels, run_copy(): pl.pallas_call(copy_kernel, out_shape=tuple((jax.ShapeDtypeStruct(a.shape...  12.6 us

profile of v8, /device:TPU:0, one launch (start us, length us, event | category | flops | bytes accessed | tf_op | source)
XLA Modules:
  0.0 252.9 jit_solution(7876685602770559414)
XLA Ops:
  0.6 239.5 %step.1 = (f32[2,96,3072]{2,1,0:T(8,128)}, f32[2,384,768]{2,1,0:T(8,128)}, f32[2,96,3072]{2,1,0:T(8,128)}, f32[2,384,768]{2,1,0:T(8,128)}, f32[2,96,3072]{2,1,0:...) custom-call(bf16[2,2048,768]{2,1,0:T(8,128)(2,1)} %bitcast.8, ...), custom_call_target="tpu_custom_call" | custom-call | tf_op jit(solution)/shard_map/step/pallas_call | solution.py:585
  240.1 12.6 %copy_out.1 = (f32[2,96,3072]{2,1,0:T(8,128)}, f32[2,384,768]{2,1,0:T(8,128)}, f32[2,96,3072]{2,1,0:T(8,128)}, f32[2,384,768]{2,1,0:T(8,128)}, f32[2,96,3072]{2,...) custom-call(f32[2,96,3072]{2,1,0:T(8,128)} %get-tuple-element.21.refs_0_, ...), custom_call_target="tpu_custom_call" | custom-call | tf_op jit(solution)/shard_map/copy_out/pallas_call | solution.py:628
